TPU v7x, 256 devices: a whole 4x4x8 slice. The times are simulated.
256 devices in a mesh: dp: 16 (over x, z_lo), cls: 16 (over y, z_hi, core).
Axes of the slice: x: 4, y: 4, z: 8 (z_hi: 2, z_lo: 4; z = z_hi * 4 + z_lo), core: 2. Of those that a mesh axis runs over, the one named last changes fastest.
Arguments:
- embeddings: bfloat16 [49152, 768], P('dp'), may hold values from -6 to 6
- labels: int32 [49152], P('dp'), may hold values from 0 to 22015, as said below
- row_count: int32 [16], P('dp'), may hold values from 768 to 3072
Outputs:
- class_means: float32 [22016, 768], P(('dp', 'cls'))
- prototypes: float32 [22016, 768], P(('dp', 'cls'))
- similarity: float32 [49152], P('dp')
Inputs may be any that keep to these rules, and one draw needn't show every extreme that they name: Rows of index i of dp at or beyond row_count[i] are padding. `labels`: classes c and c' belong to the same block when c // 86 == c' // 86; block b belongs to index b mod 16 of cls. The rows of one index of dp name at most 16 distinct classes of any one block. Some block has exactly 16 of its classes named by the rows of every index of dp. The rows of some index of dp name exactly 16 classes of every block of some index of cls.
All inputs are finite; a program needn't handle non-finite values.
Results may differ from a plain program's by a relative error of at most 0.0017.
Values sent between devices are 32-bit elements; how exact they have to be, the bound alone decides.
A program may use at most 64 MiB of HBM per device.

v0:
```python
import jax
import jax.numpy as jnp
from jax import lax
from jax.sharding import Mesh
from jax.sharding import PartitionSpec as P

CLS_DEV = 86
SLOTS = 16
DP = ("dp_0", "dp_1")
DP_CLS = ("dp_0", "dp_1", "cls")


epsilon = 1e-06
sharpness = 4.0


def whole_of(shard, axes, dim):
    whole = shard
    for number in range(len(axes) - 1, -1, -1):
        whole = lax.all_gather(whole, axes[number], axis=dim, tiled=True)
    return whole


def in_one_piece(arrays, axis, split_dim, concat_dim, along):
    columns = [a.reshape(*a.shape[:along], -1) for a in arrays]
    both = jnp.concatenate(columns, axis=along)
    whole, at, gathered = (
        lax.all_to_all(both, axis, split_axis=split_dim, concat_axis=concat_dim, tiled=True),
        0,
        [],
    )
    for a, column in zip(arrays, columns):
        slab = whole[..., at : at + column.shape[along]]
        gathered.append(slab.reshape(*slab.shape[:along], *a.shape[along:]))
        at += column.shape[along]
    return tuple(gathered)


def sent_to_all(shard, axis):
    length = lax.axis_size(axis)
    return lax.all_to_all(
        jnp.broadcast_to(shard[None], (length, *shard.shape)), axis, 0, 0, tiled=True
    )


def of_everyone(shard, axis):
    everything = sent_to_all(shard, axis)
    return jnp.sum(everything, axis=0)


def normalize(matrix):
    return matrix / jnp.sqrt(jnp.sum(matrix * matrix, axis=1, keepdims=True) + epsilon)


def slot_tables(counts, owner_count):
    present = (counts > 0).reshape(owner_count, CLS_DEV)
    rank = jnp.cumsum(present.astype(jnp.int32), axis=1) - 1
    slot_iota = lax.iota(jnp.int32, SLOTS)
    class_iota = lax.iota(jnp.int32, CLS_DEV)
    match = present[:, None, :] & (rank[:, None, :] == slot_iota[None, :, None])
    filled = jnp.any(match, axis=2)
    chosen = jnp.sum(jnp.where(match, class_iota[None, None, :], 0), axis=2)
    source = lax.iota(jnp.int32, owner_count)[:, None] * CLS_DEV + chosen
    slot_ids = jnp.where(filled, chosen.astype(jnp.float32), -1.0)
    return (source, filled, slot_ids)


def pack_rows(table, source, filled):
    picked = jnp.take(table, source.reshape(-1), axis=0).reshape(filled.shape + (table.shape[1],))
    return jnp.where(filled[:, :, None], picked, 0.0)


def spread_rows(received, received_ids):
    flat_ids = received_ids.reshape(-1)
    onehot = (flat_ids[:, None] == lax.iota(jnp.float32, CLS_DEV)[None, :]).astype(jnp.float32)
    flat_rows = received.reshape(flat_ids.shape[0], -1)
    return lax.dot_general(
        onehot,
        flat_rows,
        (((0,), (0,)), ((), ())),
        precision=lax.Precision.HIGHEST,
        preferred_element_type=jnp.float32,
    )


def gather_units(class_means):
    return whole_of(normalize(class_means), DP, 0)


def shards(embeddings, labels, row_count):
    row_total = embeddings.shape[0]
    feature_width = embeddings.shape[1]
    group_count = lax.axis_size("cls")
    owner_count = lax.axis_size(DP)
    table_width = CLS_DEV * owner_count
    tile_rows = min(512, row_total)
    position = lax.iota(jnp.int32, row_total)
    alive = position < row_count[0]
    class_group = labels // CLS_DEV
    owned = (class_group % group_count == lax.axis_index("cls")) & alive
    local_label = jnp.where(owned, class_group // group_count * CLS_DEV + labels % CLS_DEV, -1)
    turns = row_total // tile_rows
    columns = lax.iota(jnp.int32, table_width)
    nothing = jnp.zeros((), jnp.bfloat16)

    def accumulate(weights, with_counts):

        def advance(turn, state_pair):
            running, counts = state_pair
            first_row = turn * tile_rows
            row_piece = lax.dynamic_slice_in_dim(embeddings, first_row, tile_rows, 0)
            tile_labels = lax.dynamic_slice_in_dim(local_label, first_row, tile_rows, 0)
            tile_weights = lax.dynamic_slice_in_dim(weights, first_row, tile_rows, 0)
            onehot = jnp.where(
                tile_labels[:, None] == columns[None, :], tile_weights[:, None], nothing
            )
            running = running + lax.dot_general(
                onehot, row_piece, (((0,), (0,)), ((), ())), preferred_element_type=jnp.float32
            )
            if with_counts:
                counts = counts + jnp.sum(onehot.astype(jnp.float32), axis=0)
            return (running, counts)

        start_pair = (
            jnp.zeros((table_width, feature_width), jnp.float32),
            jnp.zeros((table_width,), jnp.float32),
        )
        return lax.fori_loop(0, turns, advance, start_pair)

    class_sums, counts = accumulate(jnp.ones((row_total,), jnp.bfloat16), True)
    source, filled, slot_ids = slot_tables(counts, owner_count)
    sum_slots = pack_rows(class_sums, source, filled)
    count_slots = jnp.where(
        filled, jnp.take(counts, source.reshape(-1), axis=0).reshape(filled.shape), 0.0
    )
    got_sums, got_counts, got_ids = in_one_piece((sum_slots, count_slots, slot_ids), DP, 0, 0, 2)
    own_sums = spread_rows(got_sums, got_ids)
    own_counts = spread_rows(got_counts, got_ids)[:, 0]
    class_means = own_sums / jnp.maximum(own_counts, 1.0)[:, None]
    unit_table = gather_units(class_means)
    features = embeddings.astype(jnp.float32)
    lengths = jnp.sqrt(jnp.sum(features * features, axis=1) + epsilon)
    lookup = jnp.take(unit_table, jnp.maximum(local_label, 0), axis=0)
    own_product = jnp.where(owned, jnp.sum(features * lookup, axis=1), 0.0)
    full_product = of_everyone(own_product, "cls")
    similarity = jnp.where(alive, full_product / lengths, 0.0)
    weight = jnp.where(alive, jnp.exp(sharpness * (similarity - 1.0)), 0.0).astype(jnp.bfloat16)
    weighted, unused = accumulate(weight, False)
    weighted_slots = pack_rows(weighted, source, filled)
    got_weighted, got_labels = in_one_piece((weighted_slots, slot_ids), DP, 0, 0, 2)
    own_weighted = spread_rows(got_weighted, got_labels)
    prototypes = normalize(own_weighted)
    return (class_means, prototypes, similarity)


def solution(mesh):
    split = Mesh(mesh.devices.reshape(4, 4, mesh.shape["cls"]), ("dp_0", "dp_1", "cls"))
    placed = (P(DP, None), P(DP), P(DP))
    return jax.shard_map(
        shards,
        mesh=split,
        in_specs=placed,
        out_specs=(P(DP_CLS, None), P(DP_CLS, None), P(DP)),
        check_vma=False,
    )
```

profile of v0, /device:TPU:1, one launch (start us, length us, event | category | flops | bytes accessed | tf_op | source)
XLA Modules:
  0.0 296.3 jit_solution(1393273185039919635)
XLA Ops:
  7.9 0.7 maximum_compare_fusion
  8.6 35.6 %while.30 = (s32[]{:T(128)}, f32[1376,768]{1,0:T(8,128)}, f32[1376]{0:T(1024)S(1)}, s32[3072]{0:T(1024)S(1)}, bf16[3072,768]{1,0:T(8,128)(2,1)}, /*index=5*/s32[]{:T(128)}, s32[]{:T(128)}, s32[]{:T(128)}, s32[]{:T(128)}) while((s32[]{:T(128)}, f32[1376,768]{1,0:T(8,128)}, f32[1376]{0:T(1024)S(1)}, s32[3072]{0:T(1024)S(1)}, ...), condition=%wide.region_2.3_spmd.clone, body=%wide.region_0.2_spmd.clone.sunk | while | flops 1088472320 | bytes 9270942 | solution.py:128
  8.7 0.1 dynamic_slice.50
  8.7 4.4 %select_add_fusion.6 = f32[1376,768]{1,0:T(8,128)} fusion(f32[1376,768]{1,0:T(8,128)} %get-tuple-element.374, pred[]{:T(512)S(6)} %compare.9, s32[512]{0:T(512)S(1)} %dynamic_slice.50, bf16[3072,768]{1,0:T(8,128)(2,1)} %get-tuple-element.386, s32[]{:T(128)S(6)} %select_n.232), kind=kOutput, calls=%fused_computation.6.clone.1 | convolution fusion | flops 1085652992 | bytes 9242629 | tf_op jit(solution)/shard_map/while/body/eval_jaxpr/dot_general | solution.py:117
  13.1 0.4 convert_reduce_fusion.2
  13.5 0.1 dynamic_slice.50
  13.6 5.7 %select_add_fusion.6 = f32[1376,768]{1,0:T(8,128)} fusion(f32[1376,768]{1,0:T(8,128)} %get-tuple-element.374, pred[]{:T(512)S(6)} %compare.9, s32[512]{0:T(512)S(1)} %dynamic_slice.50, bf16[3072,768]{1,0:T(8,128)(2,1)} %get-tuple-element.386, s32[]{:T(128)S(6)} %select_n.232), kind=kOutput, calls=%fused_computation.6.clone.1 | convolution fusion | flops 1085652992 | bytes 9242629 | tf_op jit(solution)/shard_map/while/body/eval_jaxpr/dot_general | solution.py:117
  19.2 0.4 convert_reduce_fusion.2
  19.6 0.1 dynamic_slice.50
  19.7 5.7 %select_add_fusion.6 = f32[1376,768]{1,0:T(8,128)} fusion(f32[1376,768]{1,0:T(8,128)} %get-tuple-element.374, pred[]{:T(512)S(6)} %compare.9, s32[512]{0:T(512)S(1)} %dynamic_slice.50, bf16[3072,768]{1,0:T(8,128)(2,1)} %get-tuple-element.386, s32[]{:T(128)S(6)} %select_n.232), kind=kOutput, calls=%fused_computation.6.clone.1 | convolution fusion | flops 1085652992 | bytes 9242629 | tf_op jit(solution)/shard_map/while/body/eval_jaxpr/dot_general | solution.py:117
  25.4 0.4 convert_reduce_fusion.2
  25.9 5.7 %select_add_fusion.6 = f32[1376,768]{1,0:T(8,128)} fusion(f32[1376,768]{1,0:T(8,128)} %get-tuple-element.374, pred[]{:T(512)S(6)} %compare.9, s32[512]{0:T(512)S(1)} %dynamic_slice.50, bf16[3072,768]{1,0:T(8,128)(2,1)} %get-tuple-element.386, s32[]{:T(128)S(6)} %select_n.232), kind=kOutput, calls=%fused_computation.6.clone.1 | convolution fusion | flops 1085652992 | bytes 9242629 | tf_op jit(solution)/shard_map/while/body/eval_jaxpr/dot_general | solution.py:117
  31.5 0.4 convert_reduce_fusion.2
  32.0 5.7 %select_add_fusion.6 = f32[1376,768]{1,0:T(8,128)} fusion(f32[1376,768]{1,0:T(8,128)} %get-tuple-element.374, pred[]{:T(512)S(6)} %compare.9, s32[512]{0:T(512)S(1)} %dynamic_slice.50, bf16[3072,768]{1,0:T(8,128)(2,1)} %get-tuple-element.386, s32[]{:T(128)S(6)} %select_n.232), kind=kOutput, calls=%fused_computation.6.clone.1 | convolution fusion | flops 1085652992 | bytes 9242629 | tf_op jit(solution)/shard_map/while/body/eval_jaxpr/dot_general | solution.py:117
  37.7 0.4 convert_reduce_fusion.2
  38.1 0.1 dynamic_slice.50
  38.2 5.7 %select_add_fusion.6 = f32[1376,768]{1,0:T(8,128)} fusion(f32[1376,768]{1,0:T(8,128)} %get-tuple-element.374, pred[]{:T(512)S(6)} %compare.9, s32[512]{0:T(512)S(1)} %dynamic_slice.50, bf16[3072,768]{1,0:T(8,128)(2,1)} %get-tuple-element.386, s32[]{:T(128)S(6)} %select_n.232), kind=kOutput, calls=%fused_computation.6.clone.1 | convolution fusion | flops 1085652992 | bytes 9242629 | tf_op jit(solution)/shard_map/while/body/eval_jaxpr/dot_general | solution.py:117
  43.8 0.4 convert_reduce_fusion.2
  44.2 0.1 and.57
  44.3 0.2 reduce_window_sum.11
  44.6 0.4 select_reduce_fusion
  45.0 0.1 add.193
  45.1 0.4 fusion.26
  45.5 0.1 add.198
  45.6 1.7 gather_fusion
  47.4 3.6 %gather_fusion.2 = f32[256,768]{1,0:T(8,128)S(1)} fusion(f32[1376,768]{1,0:T(8,128)} %get-tuple-element.224, s32[1024]{0:T(1024)S(1)} %pad_clamp_fusion.1), kind=kCustom, calls=%fused_computation.clone | custom fusion | bytes 1573888 | tf_op jit(solution)/shard_map/jit(_take)/gather | solution.py:69
  51.0 0.1 broadcast_select_fusion.1
  51.1 0.1 broadcast_select_fusion.3
  51.4 0.2 copy.18
  51.5 0.2 copy.17
  51.7 0.1 pad_maximum_fusion
  51.8 33.0 %all_to_all.16 = f32[16,16,770]{2,1,0:T(8,128)S(1)} all-to-all(f32[16,16,770]{2,1,0:T(8,128)S(1)} %pad_maximum_fusion), channel_id=1, replica_groups=mesh['dp_0'=4,'dp_1'=4,'cls'=16] {'dp_0','dp_1'}, dimensions={0} | all-to-all | bytes 1576960 | tf_op jit(solution)/shard_map/all_to_all | solution.py:28
  84.8 0.2 slice_reduce_fusion.1
  85.0 0.1 eq.130
  85.1 0.1 reshape.250
  85.2 0.2 fusion.23
  85.4 0.1 slice.29
  85.5 1.3 multiply_reduce_fusion.1
  86.8 0.8 divide_bitcast_fusion
  87.7 32.5 %all-gather.6.cloned.1.call-done = f32[4,86,768]{2,1,0:T(8,128)} async-done(((f32[1,86,768]{2,1,0:T(8,128)}), f32[4,86,768]{2,1,0:T(8,128)}) %all-gather.6.cloned.1.call-update) | async-done | bytes 1056784 | tf_op jit(solution)/shard_map/all_gather | solution.py:20
  120.2 2.4 reshape.245
  122.6 50.7 %all-gather.4.cloned.1.call-done = f32[1376,768]{1,0:T(8,128)} async-done(((f32[344,768]{1,0:T(8,128)}), f32[1376,768]{1,0:T(8,128)}) %all-gather.4.cloned.1.call-update) | async-done | bytes 4227088 | tf_op jit(solution)/shard_map/all_gather | solution.py:20
  173.3 17.7 %gather_fusion.1 = f32[3072,768]{1,0:T(8,128)} fusion(f32[1376,768]{1,0:T(8,128)} %all-gather.4.cloned.1.call-done, s32[3072]{0:T(1024)S(1)} %maximum_clamp_fusion), kind=kCustom, calls=%fused_computation.3 | custom fusion | bytes 18886656 | tf_op jit(solution)/shard_map/jit(_take)/gather | solution.py:143
  191.0 6.7 %fusion.22 = (f32[3072]{0:T(1024)S(1)}, f32[3072]{0:T(1024)S(1)}) fusion(bf16[3072,768]{1,0:T(8,128)(2,1)} %get-tuple-element.421, f32[3072,768]{1,0:T(8,128)} %gather_fusion.1, pred[3072]{0:T(1024)(128)(4,1)S(1)} %get-tuple-element.292), kind=kLoop, calls=%fused_computation.30 | loop fusion | flops 14149632 | bytes 14183424 | tf_op jit(solution)/shard_map/reduce_sum | solution.py:142
  197.7 0.8 broadcast_in_dim.158
  198.5 10.3 %all-to-all-start.1 = ((f32[16,1,3072]{2,1,0:T(1,128)}), f32[16,1,3072]{2,1,0:T(1,128)S(1)}, u32[]{:S(2)}, u32[]{:S(2)}) async-start(f32[16,1,3072]{2,1,0:T(1,128)} %broadcast_in_dim.158), calls=%async_computation.1 | async-start | bytes 393216 | tf_op jit(solution)/shard_map/all_to_all | solution.py:41
  208.8 10.7 %all-to-all-done.1 = f32[16,1,3072]{2,1,0:T(1,128)S(1)} async-done(((f32[16,1,3072]{2,1,0:T(1,128)}), f32[16,1,3072]{2,1,0:T(1,128)S(1)}, u32[]{:S(2)}, u32[]{:S(2)}) %all-to-all-start.1) | async-done | bytes 196640 | tf_op jit(solution)/shard_map/all_to_all | solution.py:41
  219.4 0.1 reduce_sum.73
  219.6 0.6 select_convert_fusion
  220.2 34.5 %while.31 = (s32[]{:T(128)}, f32[1376,768]{1,0:T(8,128)}, s32[3072]{0:T(1024)S(1)}, bf16[3072]{0:T(1024)(128)(2,1)S(1)}, bf16[3072,768]{1,0:T(8,128)(2,1)}, /*index=5*/s32[]{:T(128)}, s32[]{:T(128)}, s32[]{:T(128)}, s32[]{:T(128)}) while((s32[]{:T(128)}, f32[1376,768]{1,0:T(8,128)}, s32[3072]{0:T(1024)S(1)}, ...), condition=%wide.region_11.13_spmd.clone, body=%wide.region_10.12_spmd.clone.sunk | while | flops 1085652992 | bytes 9249953 | solution.py:128
  220.3 4.5 %select_add_fusion.8 = f32[1376,768]{1,0:T(8,128)} fusion(f32[1376,768]{1,0:T(8,128)} %get-tuple-element.401, pred[]{:T(512)S(6)} %compare.10, s32[512]{0:T(512)S(1)} %dynamic_slice.52, bf16[3072,768]{1,0:T(8,128)(2,1)} %get-tuple-element.413, s32[]{:T(128)S(6)} %select_n.234, bf16[512]{0:T(512)(128)(2,1)S(1)} %dynamic_slice.53), kind=kOutput, calls=%fused_computation.18.clone.1 | convolution fusion | flops 1085652992 | bytes 9243653 | tf_op jit(solution)/shard_map/while/body/eval_jaxpr/dot_general | solution.py:117
  225.0 5.8 %select_add_fusion.8 = f32[1376,768]{1,0:T(8,128)} fusion(f32[1376,768]{1,0:T(8,128)} %get-tuple-element.401, pred[]{:T(512)S(6)} %compare.10, s32[512]{0:T(512)S(1)} %dynamic_slice.52, bf16[3072,768]{1,0:T(8,128)(2,1)} %get-tuple-element.413, s32[]{:T(128)S(6)} %select_n.234, bf16[512]{0:T(512)(128)(2,1)S(1)} %dynamic_slice.53), kind=kOutput, calls=%fused_computation.18.clone.1 | convolution fusion | flops 1085652992 | bytes 9243653 | tf_op jit(solution)/shard_map/while/body/eval_jaxpr/dot_general | solution.py:117
  231.0 5.8 %select_add_fusion.8 = f32[1376,768]{1,0:T(8,128)} fusion(f32[1376,768]{1,0:T(8,128)} %get-tuple-element.401, pred[]{:T(512)S(6)} %compare.10, s32[512]{0:T(512)S(1)} %dynamic_slice.52, bf16[3072,768]{1,0:T(8,128)(2,1)} %get-tuple-element.413, s32[]{:T(128)S(6)} %select_n.234, bf16[512]{0:T(512)(128)(2,1)S(1)} %dynamic_slice.53), kind=kOutput, calls=%fused_computation.18.clone.1 | convolution fusion | flops 1085652992 | bytes 9243653 | tf_op jit(solution)/shard_map/while/body/eval_jaxpr/dot_general | solution.py:117
  236.9 5.8 %select_add_fusion.8 = f32[1376,768]{1,0:T(8,128)} fusion(f32[1376,768]{1,0:T(8,128)} %get-tuple-element.401, pred[]{:T(512)S(6)} %compare.10, s32[512]{0:T(512)S(1)} %dynamic_slice.52, bf16[3072,768]{1,0:T(8,128)(2,1)} %get-tuple-element.413, s32[]{:T(128)S(6)} %select_n.234, bf16[512]{0:T(512)(128)(2,1)S(1)} %dynamic_slice.53), kind=kOutput, calls=%fused_computation.18.clone.1 | convolution fusion | flops 1085652992 | bytes 9243653 | tf_op jit(solution)/shard_map/while/body/eval_jaxpr/dot_general | solution.py:117
  242.9 5.8 %select_add_fusion.8 = f32[1376,768]{1,0:T(8,128)} fusion(f32[1376,768]{1,0:T(8,128)} %get-tuple-element.401, pred[]{:T(512)S(6)} %compare.10, s32[512]{0:T(512)S(1)} %dynamic_slice.52, bf16[3072,768]{1,0:T(8,128)(2,1)} %get-tuple-element.413, s32[]{:T(128)S(6)} %select_n.234, bf16[512]{0:T(512)(128)(2,1)S(1)} %dynamic_slice.53), kind=kOutput, calls=%fused_computation.18.clone.1 | convolution fusion | flops 1085652992 | bytes 9243653 | tf_op jit(solution)/shard_map/while/body/eval_jaxpr/dot_general | solution.py:117
  248.9 5.8 %select_add_fusion.8 = f32[1376,768]{1,0:T(8,128)} fusion(f32[1376,768]{1,0:T(8,128)} %get-tuple-element.401, pred[]{:T(512)S(6)} %compare.10, s32[512]{0:T(512)S(1)} %dynamic_slice.52, bf16[3072,768]{1,0:T(8,128)(2,1)} %get-tuple-element.413, s32[]{:T(128)S(6)} %select_n.234, bf16[512]{0:T(512)(128)(2,1)S(1)} %dynamic_slice.53), kind=kOutput, calls=%fused_computation.18.clone.1 | convolution fusion | flops 1085652992 | bytes 9243653 | tf_op jit(solution)/shard_map/while/body/eval_jaxpr/dot_general | solution.py:117
  254.7 3.6 %gather_fusion.3 = f32[256,768]{1,0:T(8,128)S(1)} fusion(f32[1376,768]{1,0:T(8,128)} %get-tuple-element.225, s32[1024]{0:T(1024)S(1)} %pad_clamp_fusion.1), kind=kCustom, calls=%fused_computation.1.clone | custom fusion | bytes 1573888 | tf_op jit(solution)/shard_map/jit(_take)/gather | solution.py:69
  258.3 0.1 broadcast_select_fusion
  258.4 0.1 broadcast_select_fusion.2
  258.6 29.1 %all_to_all.17 = f32[16,16,769]{2,1,0:T(8,128)S(1)} all-to-all(f32[16,16,769]{2,1,0:T(8,128)S(1)} %pad_maximum_fusion.1), channel_id=1, replica_groups=mesh['dp_0'=4,'dp_1'=4,'cls'=16] {'dp_0','dp_1'}, dimensions={0} | all-to-all | bytes 1574912 | tf_op jit(solution)/shard_map/all_to_all | solution.py:28
  287.8 0.1 slice_reduce_fusion
  287.9 0.1 eq.134
  288.0 0.6 multiply_reduce_fusion
  288.6 0.8 broadcast_divide_fusion
  (45 shorter events, 1.7 us)
Async XLA Ops:
  7.2 113.1 %all-gather.6.cloned.1.call-start = ((), (), s32[]{:S(2)}) async-start(), calls=%async_computation.4 | async-start | bytes 1351680 | tf_op jit(solution)/shard_map/all_gather | solution.py:20
  87.7 85.7 %all-gather.4.cloned.1.call-start = ((), (), s32[]{:S(2)}) async-start(), calls=%async_computation.3 | async-start | bytes 5283840 | tf_op jit(solution)/shard_map/all_gather | solution.py:20
  198.5 21.0 %all-to-all-start.1 = ((f32[16,1,3072]{2,1,0:T(1,128)}), f32[16,1,3072]{2,1,0:T(1,128)S(1)}, u32[]{:S(2)}, u32[]{:S(2)}) async-start(f32[16,1,3072]{2,1,0:T(1,128)} %broadcast_in_dim.158), calls=%async_computation.1 | async-start | bytes 393216 | tf_op jit(solution)/shard_map/all_to_all | solution.py:41
Sparse Core Ops, SparseCore 0:
  87.8 32.3 all-gather.5
  122.8 50.5 all-gather.3
where the time goes:
time: 297 us; the launch traced here: 296 us
  waiting for transfers between devices  93.9 us (32%)
  matrix products  68.4 us (23%)
  blocking collectives  62.1 us (21%)
  local copies, waits for them, and re-layouts  32.5 us (11%)
  between operations  14.9 us (5%)
  other arithmetic  14 us (5%)
  starting transfers between devices  10.4 us (4%)
    all_gather x2, waiting for transfers between devices, whole_of(): whole = lax.all_gather(whole, axes[number], axis=dim, tiled=True)  83.2 us
    dot_general x12, matrix products, advance(): lax.dot_general(onehot, row_piece, (((0,), (0,)), ((), ())), preferred_el...  66.3 us
    all_to_all x2, blocking collectives, in_one_piece(): lax.all_to_all(both, axis, split_axis=split_dim, concat_axis=concat_dim,...  62.1 us
    gather x1, local copies, waits for them, and re-layouts, shards(): lookup = jnp.take(unit_table, jnp.maximum(local_label, 0), axis=0)  17.7 us
    all_to_all x1, waiting for transfers between devices, sent_to_all(): lax.all_to_all(jnp.broadcast_to(shard[None], (length, *shard.shape)), axi...  10.7 us
    all_to_all x1, starting transfers between devices, sent_to_all(): lax.all_to_all(jnp.broadcast_to(shard[None], (length, *shard.shape)), axi...  10.3 us
    gather x2, local copies, waits for them, and re-layouts, pack_rows(): jnp.take(table, source.reshape(-1), axis=0)  7.2 us
    reduce_sum x1, other arithmetic, shards(): lengths = jnp.sqrt(jnp.sum(features * features, axis=1) + epsilon)  6.66 us
  transfers between devices with their start and end apart: 3, of which 3 were waited for; matrix products, arithmetic and copies ran while one was open for 0% of the time, Pallas kernels for 0%

commit v1 on v0

v1 whole, which is shorter than its diff:
```python
import jax
import jax.numpy as jnp
from jax import lax
from jax.experimental import pallas as pl
from jax.experimental.pallas import tpu as pltpu
from jax.sharding import PartitionSpec as P

MESH = pl.DeviceIdType.MESH
F32 = jnp.float32
BF16 = jnp.bfloat16

CLS_DEV = 86
SLOTS = 16
PEERS = 16
TABLE = PEERS * SLOTS
LANES = 128
EPSILON = 1e-06
SHARPNESS = 4.0

X, Y, Z = 4, 4, 8
DX = [k // 4 for k in range(PEERS)]
DZ = [(0, 1, -1, 2)[k % 4] for k in range(PEERS)]


def split(value, parts):
    pieces, rest = [], value
    for number in range(parts):
        piece = rest.astype(BF16)
        pieces.append(piece)
        if number < parts - 1:
            rest = rest - piece.astype(F32)
    return pieces


def dot(a, b, contract):
    return lax.dot_general(a, b, (contract, ((), ())), preferred_element_type=F32)


NN = ((1,), (0,))
NT = ((1,), (1,))
TN = ((0,), (0,))


def ranks(present):
    before = lax.broadcasted_iota(jnp.int32, (LANES, LANES), 0)
    after = lax.broadcasted_iota(jnp.int32, (LANES, LANES), 1)
    triangle = jnp.where(before < after, 1.0, 0.0).astype(BF16)
    return dot(present.astype(BF16), triangle, NN)


def kernel(
    rc_ref,
    lab_ref,
    e_hbm,
    means_ref,
    proto_ref,
    sim_ref,
    e_ref,
    hot_ref,
    meta_out,
    meta_in,
    out1,
    in1,
    out2,
    in2,
    out3,
    in3,
    map_ref,
    part_ref,
    sim_own,
    sim_in,
    sim_half,
    sim_far,
    e_sem,
    meta_ssem,
    meta_rsem,
    ssem,
    rsem,
    sim_ssem,
    sim_rsem,
):
    rows, width = e_ref.shape
    dp, cls = lax.axis_index("dp"), lax.axis_index("cls")
    x, z_lo = dp // 4, dp % 4
    y, z_hi, core = cls // 4, (cls // 2) % 2, cls % 2
    z = z_hi * 4 + z_lo
    sign = 1 - 2 * core

    def device(x_at, y_at, z_at, core_at):
        return (x_at * 4 + z_at % 4, y_at * 4 + (z_at // 4) * 2 + core_at)

    def at_offset(dx, dz):
        return device((x + X + sign * dx) % X, y, (z + Z + sign * dz) % Z, core)

    fan = [(dy, dc) for dc in range(2) for dy in range(Y) if (dy, dc) != (0, 0)]

    def fan_device(dy, dc):
        return device(x, (y + dy) % Y, z, (core + dc) % 2)

    far = device(x, y, (z + 4) % Z, core)

    pieces = e_sem.shape[0]
    piece_rows = rows // pieces
    loads = [
        pltpu.make_async_copy(
            e_hbm.at[pl.ds(n * piece_rows, piece_rows)],
            e_ref.at[pl.ds(n * piece_rows, piece_rows)],
            e_sem.at[n],
        )
        for n in range(pieces)
    ]
    for load in loads:
        load.start()

    barrier = pltpu.get_barrier_semaphore()
    greeted = 0
    for dx in range(X):
        for dz in range(-2, 3):
            if (dx, dz) != (0, 0):
                pl.semaphore_signal(barrier, inc=1, device_id=at_offset(dx, dz), device_id_type=MESH)
                greeted += 1
    for dy, dc in fan:
        pl.semaphore_signal(barrier, inc=1, device_id=fan_device(dy, dc), device_id_type=MESH)
        greeted += 1
    pl.semaphore_signal(barrier, inc=1, device_id=far, device_id_type=MESH)
    greeted += 1

    label = lab_ref[...]
    position = lax.broadcasted_iota(jnp.int32, (1, rows), 1)
    block = (label * 48771) >> 22
    inner = label - block * CLS_DEV
    block_dp, block_cls = block >> 4, block & 15
    block_z = ((block_cls >> 1) & 1) * 4 + (block_dp & 3)
    dx = ((block_dp >> 2) - x) * sign & 3
    dz = (block_z - z) * sign & 7
    turn = jnp.where(dz == 7, 2, jnp.where(dz == 2, 3, dz))
    owned = (
        (position < rc_ref[0])
        & ((block_cls >> 2) == y)
        & ((block_cls & 1) == core)
        & ((dz <= 2) | (dz == 7))
    )
    peer = jnp.where(owned, dx * 4 + turn, -1)
    peer_iota = lax.broadcasted_iota(jnp.int32, (PEERS, rows), 0)
    inner_iota = lax.broadcasted_iota(jnp.int32, (LANES, rows), 0)
    peer_hot = jnp.where(peer == peer_iota, 1.0, 0.0)
    inner_hot = jnp.where(inner == inner_iota, 1.0, 0.0).astype(BF16)
    counts = dot(peer_hot.astype(BF16), inner_hot, NT)
    rank = ranks(jnp.where(counts > 0, 1.0, 0.0))
    ranked = dot(rank.astype(BF16), inner_hot, NN)
    rank_row = jnp.sum(peer_hot * ranked, axis=0, keepdims=True)
    slot = jnp.where(owned, peer * SLOTS + rank_row.astype(jnp.int32), -1)

    for k in range(PEERS):
        meta_out[k] = jnp.broadcast_to(counts[k : k + 1], (8, LANES))
    meta_in[0] = jnp.broadcast_to(counts[0:1], (8, LANES))

    slot_iota = lax.broadcasted_iota(jnp.int32, (TABLE, rows), 0)
    hot_ref[...] = jnp.where(slot == slot_iota, 1.0, 0.0).astype(BF16)

    pl.semaphore_wait(barrier, greeted)
    metas = {}
    for k in range(1, PEERS):
        metas[k] = pltpu.make_async_remote_copy(
            src_ref=meta_out.at[k],
            dst_ref=meta_in.at[k],
            send_sem=meta_ssem.at[k],
            recv_sem=meta_rsem.at[k],
            device_id=at_offset(DX[k], DZ[k]),
            device_id_type=MESH,
        )
        metas[k].start()

    def exchange(phase, source, target, back):
        copies = []
        for k in range(1, PEERS):
            to = at_offset(-DX[k], -DZ[k]) if back else at_offset(DX[k], DZ[k])
            copy = pltpu.make_async_remote_copy(
                src_ref=source.at[pl.ds(k * SLOTS, SLOTS)],
                dst_ref=target.at[pl.ds(k * SLOTS, SLOTS)],
                send_sem=ssem.at[phase, k],
                recv_sem=rsem.at[phase, k],
                device_id=to,
                device_id_type=MESH,
            )
            copy.start()
            copies.append(copy)
        return copies

    for load in loads:
        load.wait()
    out1[...] = dot(hot_ref[...], e_ref[...], NN)
    in1[pl.ds(0, SLOTS)] = out1[pl.ds(0, SLOTS)]
    sends1 = exchange(0, out1, in1, False)

    ones = jnp.ones((8, LANES), BF16)
    step = 512
    for n in range(rows // step):
        tile = e_ref[pl.ds(n * step, step), :].astype(F32)
        squares = tile * tile
        lanes = squares[:, 0:LANES]
        for j in range(1, width // LANES):
            lanes = lanes + squares[:, j * LANES : (j + 1) * LANES]
        total = sum(dot(ones, piece, NT) for piece in split(lanes, 3))
        part_ref[0:1, pl.ds(n * step, step)] = total[0:1]

    for k in range(1, PEERS):
        metas[k].wait()
    counts8 = meta_in[...].reshape(PEERS * 8, LANES)
    present8 = counts8 > 0
    rank8 = jnp.where(present8, ranks(jnp.where(present8, 1.0, 0.0)), -1.0).reshape(PEERS, 8, LANES)
    at8 = lax.broadcasted_iota(jnp.int32, (PEERS, 8, LANES), 1).astype(F32)
    low = jnp.where(rank8 == at8, 1.0, 0.0)
    high = jnp.where(rank8 == at8 + 8.0, 1.0, 0.0)
    map_ref[...] = jnp.concatenate([low, high], axis=1).reshape(TABLE, LANES).astype(BF16)
    eighth = jnp.full((LANES, LANES), 0.125, BF16)
    counted = sum(dot(piece, eighth, TN) for piece in split(counts8, 2))
    inverse = 1.0 / jnp.maximum(counted, 1.0)

    for copy in sends1:
        copy.wait()
    slot_map = map_ref[...]
    sums = sum(dot(slot_map, piece, TN) for piece in split(in1[...], 3))
    means = jnp.concatenate(
        [sums[:, j * LANES : (j + 1) * LANES] * inverse for j in range(width // LANES)], axis=1
    )
    means_ref[...] = means[0:CLS_DEV]
    unit = means * (1.0 / jnp.sqrt(jnp.sum(means * means, axis=1, keepdims=True) + EPSILON))
    out2[...] = sum(dot(slot_map, piece, NN) for piece in split(unit, 2))
    in2[pl.ds(0, SLOTS)] = out2[pl.ds(0, SLOTS)]
    sends2 = exchange(1, out2, in2, True)

    for copy in sends2:
        copy.wait()
    unit_high, unit_low = split(in2[...], 2)
    for n in range(rows // step):
        tile = e_ref[pl.ds(n * step, step), :]
        products = dot(unit_high, tile, NT) + dot(unit_low, tile, NT)
        slot_n = slot[:, n * step : (n + 1) * step]
        iota_n = slot_iota[:, n * step : (n + 1) * step]
        hit = slot_n == iota_n
        product = jnp.sum(jnp.where(hit, products, 0.0), axis=0, keepdims=True)
        length = jnp.sqrt(part_ref[0:1, pl.ds(n * step, step)] + EPSILON)
        mine = slot_n >= 0
        similarity = jnp.where(mine, product / length, 0.0)
        part_ref[1:2, pl.ds(n * step, step)] = similarity
        weight = jnp.where(mine, jnp.exp(SHARPNESS * (similarity - 1.0)), 0.0)
        weight = weight.astype(BF16).astype(F32)
        hot_ref[:, pl.ds(n * step, step)] = jnp.where(hit, weight, 0.0).astype(BF16)

    cut = rows // 8
    for j in range(8):
        sim_own[j : j + 1, :] = part_ref[1:2, pl.ds(j * cut, cut)]
    out3[...] = dot(hot_ref[...], e_ref[...], NN)
    in3[pl.ds(0, SLOTS)] = out3[pl.ds(0, SLOTS)]
    sends3 = exchange(2, out3, in3, False)

    spread = []
    for n, (dy, dc) in enumerate(fan):
        copy = pltpu.make_async_remote_copy(
            src_ref=sim_own,
            dst_ref=sim_in.at[n],
            send_sem=sim_ssem.at[n],
            recv_sem=sim_rsem.at[n],
            device_id=fan_device(dy, dc),
            device_id_type=MESH,
        )
        copy.start()
        spread.append(copy)
    for copy in spread:
        copy.wait()
    half = sim_own[...]
    for n in range(len(fan)):
        half = half + sim_in[n]
    sim_half[...] = half
    across = pltpu.make_async_remote_copy(
        src_ref=sim_half,
        dst_ref=sim_far,
        send_sem=sim_ssem.at[7],
        recv_sem=sim_rsem.at[7],
        device_id=far,
        device_id_type=MESH,
    )
    across.start()
    across.wait()
    both = sim_half[...] + sim_far[...]
    for j in range(8):
        sim_ref[:, pl.ds(j * cut, cut)] = both[j : j + 1, :]

    for copy in sends3:
        copy.wait()
    weighted = sum(dot(map_ref[...], piece, TN) for piece in split(in3[...], 3))
    norm = 1.0 / jnp.sqrt(jnp.sum(weighted * weighted, axis=1, keepdims=True) + EPSILON)
    proto_ref[...] = (weighted * norm)[0:CLS_DEV]


def shards(embeddings, labels, row_count):
    rows, width = embeddings.shape
    vmem = pl.BlockSpec(memory_space=pltpu.VMEM)
    table = pltpu.VMEM((TABLE, width), F32)
    line = (8, rows // 8)
    means, prototypes, similarity = pl.pallas_call(
        kernel,
        out_shape=(
            jax.ShapeDtypeStruct((CLS_DEV, width), F32),
            jax.ShapeDtypeStruct((CLS_DEV, width), F32),
            jax.ShapeDtypeStruct((1, rows), F32),
        ),
        in_specs=[
            pl.BlockSpec(memory_space=pltpu.SMEM),
            vmem,
            pl.BlockSpec(memory_space=pl.ANY),
        ],
        out_specs=(vmem, vmem, vmem),
        scratch_shapes=[
            pltpu.VMEM((rows, width), BF16),
            pltpu.VMEM((TABLE, rows), BF16),
            pltpu.VMEM((PEERS, 8, LANES), F32),
            pltpu.VMEM((PEERS, 8, LANES), F32),
            table,
            table,
            table,
            table,
            table,
            table,
            pltpu.VMEM((TABLE, LANES), BF16),
            pltpu.VMEM((8, rows), F32),
            pltpu.VMEM(line, F32),
            pltpu.VMEM((7, *line), F32),
            pltpu.VMEM(line, F32),
            pltpu.VMEM(line, F32),
            pltpu.SemaphoreType.DMA((6,)),
            pltpu.SemaphoreType.DMA((PEERS,)),
            pltpu.SemaphoreType.DMA((PEERS,)),
            pltpu.SemaphoreType.DMA((3, PEERS)),
            pltpu.SemaphoreType.DMA((3, PEERS)),
            pltpu.SemaphoreType.DMA((8,)),
            pltpu.SemaphoreType.DMA((8,)),
        ],
        compiler_params=pltpu.CompilerParams(
            collective_id=0, has_side_effects=True, vmem_limit_bytes=56 * 1024 * 1024
        ),
    )(row_count, labels.reshape(1, rows), embeddings)
    return means, prototypes, similarity.reshape(rows)


def solution(mesh):
    return jax.shard_map(
        shards,
        mesh=mesh,
        in_specs=(P("dp", None), P("dp"), P("dp")),
        out_specs=(P(("dp", "cls"), None), P(("dp", "cls"), None), P("dp")),
        check_vma=False,
    )
```

time: 297 us -> 61.2 us (0.21)
  waiting for transfers between devices: 93.9 us -> 0 us
  matrix products: 68.4 us -> 0 us
  blocking collectives: 62.1 us -> 0 us
  Pallas kernels: 0 us -> 55 us
  local copies, waits for them, and re-layouts: 32.5 us -> 4.66 us
  other arithmetic: 14 us -> 0 us
  between operations: 14.9 us -> 1.29 us
  starting transfers between devices: 10.4 us -> 0 us
    all_gather x2 -> x0, waiting for transfers between devices: 83.2 us -> none  [whole_of(): whole = lax.all_gather(whole, axes[number], axis=dim, tiled=True)]
    dot_general x15 -> x0, matrix products: 68.4 us -> none  [the longest x12 66.3 us: advance(): lax.dot_general(onehot, row_piece, (((0,), (0,)), ((), ())), preferred_el...]
    all_to_all x2 -> x0, blocking collectives: 62.1 us -> none  [in_one_piece(): lax.all_to_all(both, axis, split_axis=split_dim, concat_axis=concat_dim,...]
    pallas_call x0 -> x1, Pallas kernels: none -> 55 us  [shards(): pl.pallas_call(kernel, out_shape=(jax.ShapeDtypeStruct((CLS_DEV, width),...]
    gather x5 -> x0, local copies, waits for them, and re-layouts: 26.7 us -> none  [the longest x1 17.7 us: shards(): lookup = jnp.take(unit_table, jnp.maximum(local_label, 0), axis=0)]
    all_to_all x1 -> x0, waiting for transfers between devices: 10.7 us -> none  [sent_to_all(): lax.all_to_all(jnp.broadcast_to(shard[None], (length, *shard.shape)), axi...]
    all_to_all x1 -> x0, starting transfers between devices: 10.3 us -> none  [sent_to_all(): lax.all_to_all(jnp.broadcast_to(shard[None], (length, *shard.shape)), axi...]
    reduce_sum x9 -> x0, other arithmetic: 9.42 us -> none  [the longest x1 6.66 us: shards(): lengths = jnp.sqrt(jnp.sum(features * features, axis=1) + epsilon)]
  transfers between devices with their start and end apart: 3 -> 0, of which waited for: 3 -> 0; matrix products, arithmetic and copies ran while one was open for 0% -> 0% of each run, Pallas kernels for 0% -> 0%
where the time goes in v1:
time: 61.2 us; the launch traced here: 60.9 us
  Pallas kernels  55 us (90%)
  local copies, waits for them, and re-layouts  4.66 us (8%)
  between operations  1.29 us (2%)
    pallas_call x1, Pallas kernels, shards(): pl.pallas_call(kernel, out_shape=(jax.ShapeDtypeStruct((CLS_DEV, width),...  55 us
    unnamed x3, local copies, waits for them, and re-layouts  4.66 us

profile of v1, /device:TPU:1, one launch (start us, length us, event | category | flops | bytes accessed | tf_op | source)
XLA Modules:
  0.0 60.9 jit_solution(12550149572666141678)
XLA Ops:
  1.3 55.0 %shard_map.58 = (f32[86,768]{1,0:T(8,128)}, f32[86,768]{1,0:T(8,128)}, f32[1,3072]{1,0:T(1,128)}) custom-call(s32[1]{0:T(128)S(6)} %copy.9.rc_ref, s32[1,3072]{1,0:T(1,128)} %bitcast.3, bf16[3072,768]{1,0:T(8,128)(2,1)} %e_hbm.1), custom_call_target="tpu_custom_call" | custom-call | tf_op jit(solution)/shard_map/pallas_call | solution.py:302
  56.3 1.7 %copy.10 = f32[86,768]{1,0:T(8,128)} copy(f32[86,768]{1,0:T(8,128)} %get-tuple-element.12) | data formatting | bytes 528384
  58.0 1.7 %copy.11 = f32[86,768]{1,0:T(8,128)} copy(f32[86,768]{1,0:T(8,128)} %get-tuple-element.13) | data formatting | bytes 528384
  59.6 1.3 %copy.12 = f32[3072]{0:T(1024)} copy(f32[3072]{0:T(1024)} %bitcast.2) | data formatting | bytes 24576

commit v2 on v1

v2 whole, which is shorter than its diff:
```python
import jax
import jax.numpy as jnp
from jax import lax
from jax.experimental import pallas as pl
from jax.experimental.pallas import tpu as pltpu
from jax.sharding import PartitionSpec as P

MESH = pl.DeviceIdType.MESH
F32 = jnp.float32
BF16 = jnp.bfloat16

CLS_DEV = 86
SLOTS = 16
PEERS = 16
TABLE = PEERS * SLOTS
LANES = 128
EPSILON = 1e-06
SHARPNESS = 4.0

X, Y, Z = 4, 4, 8
DX = [(0, 2, 1, 3)[k // 4] for k in range(PEERS)]
DZ = [(0, 1, -1, 2)[k % 4] for k in range(PEERS)]
HALF = PEERS // 2
GROUPS = ((7, 5, 6, 4, 3, 1, 2), (11, 15, 9, 13, 10, 14, 8, 12))
ORDER = (7, 11, 15, 5, 6, 3, 9, 13, 10, 14, 4, 8, 12, 1, 2)
CHUNK = 256
STEP = 512

NN = ((1,), (0,))
NT = ((1,), (1,))
TN = ((0,), (0,))


def split(value, parts):
    pieces, rest = [], value
    for number in range(parts):
        piece = rest.astype(BF16)
        pieces.append(piece)
        if number < parts - 1:
            rest = rest - piece.astype(F32)
    return pieces


def dot(a, b, contract):
    return lax.dot_general(a, b, (contract, ((), ())), preferred_element_type=F32)


def ranks(present):
    before = lax.broadcasted_iota(jnp.int32, (LANES, LANES), 0)
    after = lax.broadcasted_iota(jnp.int32, (LANES, LANES), 1)
    triangle = jnp.where(before < after, 1.0, 0.0).astype(BF16)
    return dot(present.astype(BF16), triangle, NN)


def kernel(
    rc_ref,
    lab_hbm,
    e_hbm,
    means_ref,
    proto_ref,
    sim_ref,
    lab_ref,
    e_ref,
    hot_ref,
    meta_out,
    meta_in,
    out1,
    in1,
    out2,
    in2,
    out3,
    in3,
    score_ref,
    map_ref,
    turned_ref,
    part_ref,
    sim_own,
    sim_in,
    sim_half,
    sim_far,
    small_sem,
    e_sem,
    meta_ssem,
    meta_rsem,
    ssem,
    rsem,
    sim_ssem,
    sim_rsem,
):
    rows, width = e_ref.shape
    chunks = width // CHUNK
    dp, cls = lax.axis_index("dp"), lax.axis_index("cls")
    x, z_lo = dp // 4, dp % 4
    y, z_hi, core = cls // 4, (cls // 2) % 2, cls % 2
    z = z_hi * 4 + z_lo
    sign = 1 - 2 * core

    def device(x_at, y_at, z_at, core_at):
        return (x_at * 4 + z_at % 4, y_at * 4 + (z_at // 4) * 2 + core_at)

    def at_offset(dx, dz):
        return device((x + X + sign * dx) % X, y, (z + Z + sign * dz) % Z, core)

    fan = [(dy, dc) for dc in range(2) for dy in range(Y) if (dy, dc) != (0, 0)]

    def fan_device(dy, dc):
        return device(x, (y + dy) % Y, z, (core + dc) % 2)

    far = device(x, y, (z + 4) % Z, core)

    smalls = [pltpu.make_async_copy(lab_hbm, lab_ref, small_sem.at[0])]
    pieces = e_sem.shape[0]
    piece_rows = rows // pieces
    loads = [
        pltpu.make_async_copy(
            e_hbm.at[pl.ds(n * piece_rows, piece_rows)],
            e_ref.at[pl.ds(n * piece_rows, piece_rows)],
            e_sem.at[n],
        )
        for n in range(pieces)
    ]
    for load in smalls + loads:
        load.start()

    barrier = pltpu.get_barrier_semaphore()
    greeted = 0
    for dx in range(X):
        for dz in range(-2, 3):
            if (dx, dz) != (0, 0):
                pl.semaphore_signal(barrier, inc=1, device_id=at_offset(dx, dz), device_id_type=MESH)
                greeted += 1
    for dy, dc in fan:
        pl.semaphore_signal(barrier, inc=1, device_id=fan_device(dy, dc), device_id_type=MESH)
        greeted += 1
    pl.semaphore_signal(barrier, inc=1, device_id=far, device_id_type=MESH)
    greeted += 1

    for load in smalls:
        load.wait()
    label = lab_ref[...]
    position = lax.broadcasted_iota(jnp.int32, (1, rows), 1)
    block = (label * 48771) >> 22
    inner = label - block * CLS_DEV
    block_dp, block_cls = block >> 4, block & 15
    block_z = ((block_cls >> 1) & 1) * 4 + (block_dp & 3)
    dx = ((block_dp >> 2) - x) * sign & 3
    dx = ((dx & 1) << 1) | (dx >> 1)
    dz = (block_z - z) * sign & 7
    turn = jnp.where(dz == 7, 2, jnp.where(dz == 2, 3, dz))
    owned = (
        (position < rc_ref[0])
        & ((block_cls >> 2) == y)
        & ((block_cls & 1) == core)
        & ((dz <= 2) | (dz == 7))
    )
    peer = jnp.where(owned, dx * 4 + turn, -1)
    peer_iota = lax.broadcasted_iota(jnp.int32, (PEERS, rows), 0)
    inner_iota = lax.broadcasted_iota(jnp.int32, (LANES, rows), 0)
    peer_hot = jnp.where(peer == peer_iota, 1.0, 0.0)
    inner_hot = jnp.where(inner == inner_iota, 1.0, 0.0).astype(BF16)
    counts = dot(peer_hot.astype(BF16), inner_hot, NT)
    rank = ranks(jnp.where(counts > 0, 1.0, 0.0))
    ranked = dot(rank.astype(BF16), inner_hot, NN)
    rank_row = jnp.sum(peer_hot * ranked, axis=0, keepdims=True)
    slot = jnp.where(owned, peer * SLOTS + rank_row.astype(jnp.int32), -1)

    for k in range(PEERS):
        meta_out[k] = jnp.broadcast_to(counts[k : k + 1], (8, LANES))
    meta_in[0] = jnp.broadcast_to(counts[0:1], (8, LANES))

    slot_iota = lax.broadcasted_iota(jnp.int32, (TABLE, STEP), 0)
    for n in range(rows // STEP):
        hit = slot[:, n * STEP : (n + 1) * STEP] == slot_iota
        hot_ref[:, pl.ds(n * STEP, STEP)] = jnp.where(hit, 1.0, 0.0).astype(BF16)

    pl.semaphore_wait(barrier, greeted)
    metas = {}
    for k in ORDER:
        metas[k] = pltpu.make_async_remote_copy(
            src_ref=meta_out.at[k],
            dst_ref=meta_in.at[k],
            send_sem=meta_ssem.at[k],
            recv_sem=meta_rsem.at[k],
            device_id=at_offset(DX[k], DZ[k]),
            device_id_type=MESH,
        )
        metas[k].start()

    moves = {}

    def send(phase, f, k):
        source, target = ((out1, in1), (out2, in2), (out3, in3))[phase]
        to = at_offset(-DX[k], -DZ[k]) if phase == 1 else at_offset(DX[k], DZ[k])
        move = pltpu.make_async_remote_copy(
            src_ref=source.at[f, pl.ds(k * SLOTS, SLOTS)],
            dst_ref=target.at[f, pl.ds(k * SLOTS, SLOTS)],
            send_sem=ssem.at[phase, f, k],
            recv_sem=rsem.at[phase, f, k],
            device_id=to,
            device_id_type=MESH,
        )
        move.start()
        moves[phase, f, k] = move

    def receive(phase, f, peers):
        for k in peers:
            moves[phase, f, k].wait_recv()

    def columns(f):
        return pl.ds(f * CHUNK, CHUNK)

    for load in loads:
        load.wait()
    for f in range(chunks):
        out1[f] = dot(hot_ref[...], e_ref[:, columns(f)], NN)
        in1[f, 0:SLOTS] = out1[f, 0:SLOTS]
        for k in ORDER:
            send(0, f, k)

    ones = jnp.ones((8, LANES), BF16)
    for n in range(rows // STEP):
        tile = e_ref[pl.ds(n * STEP, STEP), :].astype(F32)
        squares = tile * tile
        lanes = squares[:, 0:LANES]
        for j in range(1, width // LANES):
            lanes = lanes + squares[:, j * LANES : (j + 1) * LANES]
        total = sum(dot(ones, piece, NT) for piece in split(lanes, 3))
        part_ref[0:1, pl.ds(n * STEP, STEP)] = 1.0 / jnp.sqrt(total[0:1] + EPSILON)

    for k in ORDER:
        metas[k].wait()
    counts8 = meta_in[...].reshape(PEERS * 8, LANES)
    present8 = counts8 > 0
    rank8 = jnp.where(present8, ranks(jnp.where(present8, 1.0, 0.0)), -1.0).reshape(PEERS, 8, LANES)
    at8 = lax.broadcasted_iota(jnp.int32, (PEERS, 8, LANES), 1).astype(F32)
    low = jnp.where(rank8 == at8, 1.0, 0.0)
    high = jnp.where(rank8 == at8 + 8.0, 1.0, 0.0)
    slot_map = jnp.concatenate([low, high], axis=1).reshape(TABLE, LANES)
    map_ref[...] = slot_map.astype(BF16)
    turned_ref[...] = slot_map.T.astype(BF16)
    eighth = jnp.full((LANES, LANES), 0.125, BF16)
    counted = sum(dot(piece, eighth, TN) for piece in split(counts8, 2))
    inverse = 1.0 / jnp.maximum(counted, 1.0)

    for f in range(chunks):
        receive(0, f, ORDER)
        sums = sum(dot(turned_ref[...], piece, NN) for piece in split(in1[f], 3))
        means = jnp.concatenate(
            [sums[:, j * LANES : (j + 1) * LANES] * inverse for j in range(CHUNK // LANES)], axis=1
        )
        means_ref[:, columns(f)] = means[0:CLS_DEV]
        out2[f] = sum(dot(map_ref[...], piece, NN) for piece in split(means, 2))
        in2[f, 0:SLOTS] = out2[f, 0:SLOTS]
        for k in GROUPS[0]:
            send(1, f, k)
        for late in ((), (0,), (1, 2))[f]:
            for k in GROUPS[1]:
                send(1, late, k)

    def products(g, f, n):
        high, low = split(in2[f, pl.ds(g * LANES, LANES)], 2)
        both = jnp.concatenate([high, low], axis=0)
        found = dot(both, e_ref[pl.ds(n * STEP, STEP), columns(f)], NT)
        return found[0:LANES] + found[LANES:]

    def weigh(g):
        square = sum(
            jnp.sum(in2[f, pl.ds(g * LANES, LANES)] * in2[f, pl.ds(g * LANES, LANES)], axis=1, keepdims=True)
            for f in range(chunks)
        )
        scale = 1.0 / jnp.sqrt(square + EPSILON)
        iota = lax.broadcasted_iota(jnp.int32, (LANES, STEP), 0) + g * LANES
        for n in range(rows // STEP):
            at = pl.ds(n * STEP, STEP)
            score = (score_ref[g, :, at] + products(g, chunks - 1, n)) * scale
            slot_n = slot[:, n * STEP : (n + 1) * STEP]
            hit = slot_n == iota
            product = jnp.sum(jnp.where(hit, score, 0.0), axis=0, keepdims=True)
            mine = (slot_n >= g * LANES) & (slot_n < (g + 1) * LANES)
            similarity = jnp.where(mine, product * part_ref[0:1, at], 0.0)
            if g == 0:
                part_ref[1:2, at] = similarity
            else:
                part_ref[1:2, at] = part_ref[1:2, at] + similarity
            weight = jnp.where(mine, jnp.exp(SHARPNESS * (similarity - 1.0)), 0.0)
            weight = weight.astype(BF16).astype(F32)
            hot_ref[pl.ds(g * LANES, LANES), at] = jnp.where(hit, weight, 0.0).astype(BF16)

    def weighted_sums(g, f):
        own = pl.ds(g * LANES, LANES)
        out3[f, own] = dot(hot_ref[own, :], e_ref[:, columns(f)], NN)
        if g == 0:
            in3[f, 0:SLOTS] = out3[f, 0:SLOTS]
        for k in GROUPS[g]:
            send(2, f, k)

    def gather(g, f):
        receive(1, f, GROUPS[g])
        if f == chunks - 1:
            weigh(g)
        else:
            for n in range(rows // STEP):
                at = pl.ds(n * STEP, STEP)
                found = products(g, f, n)
                score_ref[g, :, at] = found if f == 0 else score_ref[g, :, at] + found

    gather(0, 0)
    gather(0, 1)
    gather(1, 0)
    gather(0, 2)
    for f in range(chunks):
        weighted_sums(0, f)
    gather(1, 1)
    gather(1, 2)

    cut = rows // 8
    for j in range(8):
        sim_own[j : j + 1, :] = part_ref[1:2, pl.ds(j * cut, cut)]
    weighted_sums(1, 0)
    spread = []
    for n, (dy, dc) in enumerate(fan):
        copy = pltpu.make_async_remote_copy(
            src_ref=sim_own,
            dst_ref=sim_in.at[n],
            send_sem=sim_ssem.at[n],
            recv_sem=sim_rsem.at[n],
            device_id=fan_device(dy, dc),
            device_id_type=MESH,
        )
        copy.start()
        spread.append(copy)
    weighted_sums(1, 1)
    weighted_sums(1, 2)
    for copy in spread:
        copy.wait()
    half = sim_own[...]
    for n in range(len(fan)):
        half = half + sim_in[n]
    sim_half[...] = half
    across = pltpu.make_async_remote_copy(
        src_ref=sim_half,
        dst_ref=sim_far,
        send_sem=sim_ssem.at[7],
        recv_sem=sim_rsem.at[7],
        device_id=far,
        device_id_type=MESH,
    )
    across.start()

    def merged(g, f):
        receive(2, f, GROUPS[g])
        own = pl.ds(g * LANES, LANES)
        return sum(dot(turned_ref[:, own], piece, NN) for piece in split(in3[f, own], 3))

    for f in range(chunks):
        score_ref[0, :, columns(f)] = merged(0, f)
    weighted = []
    for f in range(chunks):
        weighted.append(score_ref[0, :, columns(f)] + merged(1, f))
    square = sum(jnp.sum(piece * piece, axis=1, keepdims=True) for piece in weighted)
    norm = 1.0 / jnp.sqrt(square + EPSILON)
    for f in range(chunks):
        proto_ref[:, columns(f)] = (weighted[f] * norm)[0:CLS_DEV]

    across.wait()
    both = sim_half[...] + sim_far[...]
    for j in range(8):
        sim_ref[:, pl.ds(j * cut, cut)] = both[j : j + 1, :]
    for move in moves.values():
        move.wait_send()


def writer(means_ref, proto_ref, sim_ref, means_hbm, proto_hbm, sim_hbm, sem):
    copies = [
        pltpu.make_async_copy(means_ref, means_hbm, sem.at[0]),
        pltpu.make_async_copy(proto_ref, proto_hbm, sem.at[1]),
        pltpu.make_async_copy(sim_ref, sim_hbm, sem.at[2]),
    ]
    for copy in copies:
        copy.start()
    for copy in copies:
        copy.wait()


def shards(embeddings, labels, row_count):
    rows, width = embeddings.shape
    chunks = width // CHUNK
    vmem = pl.BlockSpec(memory_space=pltpu.VMEM)
    anywhere = pl.BlockSpec(memory_space=pl.ANY)
    hbm = pl.BlockSpec(memory_space=pltpu.MemorySpace.HBM)
    table = pltpu.VMEM((chunks, TABLE, CHUNK), F32)
    line = (8, rows // 8)
    shapes = ((CLS_DEV, width), (CLS_DEV, width), (1, rows))
    inputs = [row_count] + [
        pltpu.with_memory_space_constraint(a, pltpu.MemorySpace.HBM)
        for a in (labels.reshape(1, rows), embeddings)
    ]
    results = pl.pallas_call(
        kernel,
        out_shape=tuple(pltpu.VMEM(shape, F32) for shape in shapes),
        in_specs=[pl.BlockSpec(memory_space=pltpu.SMEM), hbm, hbm],
        out_specs=(vmem, vmem, vmem),
        scratch_shapes=[
            pltpu.VMEM((1, rows), jnp.int32),
            pltpu.VMEM((rows, width), BF16),
            pltpu.VMEM((TABLE, rows), BF16),
            pltpu.VMEM((PEERS, 8, LANES), F32),
            pltpu.VMEM((PEERS, 8, LANES), F32),
            table,
            table,
            table,
            table,
            table,
            table,
            pltpu.VMEM((2, LANES, rows), F32),
            pltpu.VMEM((TABLE, LANES), BF16),
            pltpu.VMEM((LANES, TABLE), BF16),
            pltpu.VMEM((8, rows), F32),
            pltpu.VMEM(line, F32),
            pltpu.VMEM((7, *line), F32),
            pltpu.VMEM(line, F32),
            pltpu.VMEM(line, F32),
            pltpu.SemaphoreType.DMA((2,)),
            pltpu.SemaphoreType.DMA((6,)),
            pltpu.SemaphoreType.DMA((PEERS,)),
            pltpu.SemaphoreType.DMA((PEERS,)),
            pltpu.SemaphoreType.DMA((3, chunks, PEERS)),
            pltpu.SemaphoreType.DMA((3, chunks, PEERS)),
            pltpu.SemaphoreType.DMA((8,)),
            pltpu.SemaphoreType.DMA((8,)),
        ],
        compiler_params=pltpu.CompilerParams(
            collective_id=0, has_side_effects=True, vmem_limit_bytes=48 * 1024 * 1024
        ),
    )(*inputs)
    results = [pltpu.with_memory_space_constraint(r, pltpu.MemorySpace.VMEM) for r in results]
    means, prototypes, similarity = pl.pallas_call(
        writer,
        out_shape=tuple(jax.ShapeDtypeStruct(shape, F32) for shape in shapes),
        in_specs=[vmem, vmem, vmem],
        out_specs=(anywhere, anywhere, anywhere),
        scratch_shapes=[pltpu.SemaphoreType.DMA((3,))],
    )(*results)
    return means, prototypes, similarity.reshape(rows)


def solution(mesh):
    return jax.shard_map(
        shards,
        mesh=mesh,
        in_specs=(P("dp", None), P("dp"), P("dp")),
        out_specs=(P(("dp", "cls"), None), P(("dp", "cls"), None), P("dp")),
        check_vma=False,
    )
```

time: 61.2 us -> 47.8 us (0.78)
  Pallas kernels: 55 us -> 46.4 us
  local copies, waits for them, and re-layouts: 4.66 us -> 0 us
    pallas_call x1 -> x2, Pallas kernels: 55 us -> 46.4 us  [the longest x1 45.5 us: shards(): pl.pallas_call(kernel, out_shape=tuple((pltpu.VMEM(shape, F32) for shape...]
    unnamed x3 -> x0, local copies, waits for them, and re-layouts: 4.66 us -> none
where the time goes in v2:
time: 47.8 us; the launch traced here: 47.7 us
  Pallas kernels  46.4 us (97%)
  between operations  1.28 us (3%)
    pallas_call x1, Pallas kernels, shards(): pl.pallas_call(kernel, out_shape=tuple((pltpu.VMEM(shape, F32) for shape...  45.5 us

profile of v2, /device:TPU:1, one launch (start us, length us, event | category | flops | bytes accessed | tf_op | source)
XLA Modules:
  0.0 47.7 jit_solution(4774231637785341204)
XLA Ops:
  1.3 45.5 %shard_map.58 = (f32[86,768]{1,0:T(8,128)S(1)}, f32[86,768]{1,0:T(8,128)S(1)}, f32[1,3072]{1,0:T(1,128)S(1)}) custom-call(s32[1]{0:T(128)S(6)} %copy.6.rc_ref, s32[1,3072]{1,0:T(1,128)} %bitcast.2, bf16[3072,768]{1,0:T(8,128)(2,1)} %e_hbm.1), custom_call_target="tpu_custom_call" | custom-call | tf_op jit(solution)/shard_map/pallas_call | solution.py:398
  46.8 0.8 %shard_map.59 = (f32[86,768]{1,0:T(8,128)}, f32[86,768]{1,0:T(8,128)}, f32[1,3072]{1,0:T(1,128)}) custom-call(f32[86,768]{1,0:T(8,128)S(1)} %get-tuple-element.9.means_ref, f32[86,768]{1,0:T(8,128)S(1)} %get-tuple-element.10.proto_ref, f32[1,3072]{1,0:T(1,128)S(1)} %get-tuple-element.11.sim_ref), custom_call_target="tpu_custom_call" | custom-call | tf_op jit(solution)/shard_map/pallas_call | solution.py:437

commit v3 on v2

--- a/solution.py
+++ b/solution.py
@@ -24,6 +24,7 @@
 GROUPS = ((7, 5, 6, 4, 3, 1, 2), (11, 15, 9, 13, 10, 14, 8, 12))
 ORDER = (7, 11, 15, 5, 6, 3, 9, 13, 10, 14, 4, 8, 12, 1, 2)
 CHUNK = 256
+SECOND_AT = ((), (0,), (1, 2), ())
 STEP = 512
 
 NN = ((1,), (0,))
@@ -109,17 +110,15 @@
     far = device(x, y, (z + 4) % Z, core)
 
     smalls = [pltpu.make_async_copy(lab_hbm, lab_ref, small_sem.at[0])]
-    pieces = e_sem.shape[0]
-    piece_rows = rows // pieces
     loads = [
         pltpu.make_async_copy(
-            e_hbm.at[pl.ds(n * piece_rows, piece_rows)],
-            e_ref.at[pl.ds(n * piece_rows, piece_rows)],
-            e_sem.at[n],
-        )
-        for n in range(pieces)
+            e_hbm.at[:, pl.ds(f * CHUNK, CHUNK)],
+            e_ref.at[:, pl.ds(f * CHUNK, CHUNK)],
+            e_sem.at[f],
+        )
+        for f in range(chunks)
     ]
-    for load in smalls + loads:
+    for load in smalls:
         load.start()
 
     barrier = pltpu.get_barrier_semaphore()
@@ -134,6 +133,9 @@
         greeted += 1
     pl.semaphore_signal(barrier, inc=1, device_id=far, device_id_type=MESH)
     greeted += 1
+
+    for load in loads:
+        load.start()
 
     for load in smalls:
         load.wait()
@@ -173,6 +175,34 @@
         hit = slot[:, n * STEP : (n + 1) * STEP] == slot_iota
         hot_ref[:, pl.ds(n * STEP, STEP)] = jnp.where(hit, 1.0, 0.0).astype(BF16)
 
+    moves = {}
+
+    def send(phase, f, k):
+        source, target = ((out1, in1), (out2, in2), (out3, in3))[phase]
+        to = at_offset(-DX[k], -DZ[k]) if phase == 1 else at_offset(DX[k], DZ[k])
+        move = pltpu.make_async_remote_copy(
+            src_ref=source.at[f, pl.ds(k * SLOTS, SLOTS)],
+            dst_ref=target.at[f, pl.ds(k * SLOTS, SLOTS)],
+            send_sem=ssem.at[phase, f, k],
+            recv_sem=rsem.at[phase, f, k],
+            device_id=to,
+            device_id_type=MESH,
+        )
+        move.start()
+        moves[phase, f, k] = move
+
+    def receive(phase, f, peers):
+        for k in peers:
+            moves[phase, f, k].wait_recv()
+
+    def columns(f):
+        return pl.ds(f * CHUNK, CHUNK)
+
+    def segment_sums(slots, f):
+        return dot(hot_ref[slots, :], e_ref[:, columns(f)], NN)
+
+    loads[0].wait()
+    out1[0] = segment_sums(slice(0, TABLE), 0)
     pl.semaphore_wait(barrier, greeted)
     metas = {}
     for k in ORDER:
@@ -185,34 +215,10 @@
             device_id_type=MESH,
         )
         metas[k].start()
-
-    moves = {}
-
-    def send(phase, f, k):
-        source, target = ((out1, in1), (out2, in2), (out3, in3))[phase]
-        to = at_offset(-DX[k], -DZ[k]) if phase == 1 else at_offset(DX[k], DZ[k])
-        move = pltpu.make_async_remote_copy(
-            src_ref=source.at[f, pl.ds(k * SLOTS, SLOTS)],
-            dst_ref=target.at[f, pl.ds(k * SLOTS, SLOTS)],
-            send_sem=ssem.at[phase, f, k],
-            recv_sem=rsem.at[phase, f, k],
-            device_id=to,
-            device_id_type=MESH,
-        )
-        move.start()
-        moves[phase, f, k] = move
-
-    def receive(phase, f, peers):
-        for k in peers:
-            moves[phase, f, k].wait_recv()
-
-    def columns(f):
-        return pl.ds(f * CHUNK, CHUNK)
-
-    for load in loads:
-        load.wait()
-    for f in range(chunks):
-        out1[f] = dot(hot_ref[...], e_ref[:, columns(f)], NN)
+    for f in range(chunks):
+        if f > 0:
+            loads[f].wait()
+            out1[f] = segment_sums(slice(0, TABLE), f)
         in1[f, 0:SLOTS] = out1[f, 0:SLOTS]
         for k in ORDER:
             send(0, f, k)
@@ -253,7 +259,7 @@
         in2[f, 0:SLOTS] = out2[f, 0:SLOTS]
         for k in GROUPS[0]:
             send(1, f, k)
-        for late in ((), (0,), (1, 2))[f]:
+        for late in SECOND_AT[f]:
             for k in GROUPS[1]:
                 send(1, late, k)
 
@@ -287,8 +293,8 @@
             hot_ref[pl.ds(g * LANES, LANES), at] = jnp.where(hit, weight, 0.0).astype(BF16)
 
     def weighted_sums(g, f):
-        own = pl.ds(g * LANES, LANES)
-        out3[f, own] = dot(hot_ref[own, :], e_ref[:, columns(f)], NN)
+        own = slice(g * LANES, (g + 1) * LANES)
+        out3[f, own] = segment_sums(own, f)
         if g == 0:
             in3[f, 0:SLOTS] = out3[f, 0:SLOTS]
         for k in GROUPS[g]:
@@ -306,6 +312,9 @@
 
     gather(0, 0)
     gather(0, 1)
+    for late in SECOND_AT[chunks]:
+        for k in GROUPS[1]:
+            send(1, late, k)
     gather(1, 0)
     gather(0, 2)
     for f in range(chunks):
@@ -316,7 +325,6 @@
     cut = rows // 8
     for j in range(8):
         sim_own[j : j + 1, :] = part_ref[1:2, pl.ds(j * cut, cut)]
-    weighted_sums(1, 0)
     spread = []
     for n, (dy, dc) in enumerate(fan):
         copy = pltpu.make_async_remote_copy(
@@ -329,6 +337,7 @@
         )
         copy.start()
         spread.append(copy)
+    weighted_sums(1, 0)
     weighted_sums(1, 1)
     weighted_sums(1, 2)
     for copy in spread:
@@ -421,7 +430,7 @@
             pltpu.VMEM(line, F32),
             pltpu.VMEM(line, F32),
             pltpu.SemaphoreType.DMA((2,)),
-            pltpu.SemaphoreType.DMA((6,)),
+            pltpu.SemaphoreType.DMA((chunks,)),
             pltpu.SemaphoreType.DMA((PEERS,)),
             pltpu.SemaphoreType.DMA((PEERS,)),
             pltpu.SemaphoreType.DMA((3, chunks, PEERS)),

time: 47.8 us -> 46.5 us (0.973)
  Pallas kernels: 46.4 us -> 45 us
    pallas_call x1, Pallas kernels: 45.5 us -> 44.2 us  [shards(): pl.pallas_call(kernel, out_shape=tuple((pltpu.VMEM(shape, F32) for shape...]
where the time goes in v3:
time: 46.5 us; the launch traced here: 46.3 us
  Pallas kernels  45 us (97%)
  between operations  1.28 us (3%)
    pallas_call x1, Pallas kernels, shards(): pl.pallas_call(kernel, out_shape=tuple((pltpu.VMEM(shape, F32) for shape...  44.2 us

profile of v3, /device:TPU:1, one launch (start us, length us, event | category | flops | bytes accessed | tf_op | source)
XLA Modules:
  0.0 46.3 jit_solution(3528912289968307864)
XLA Ops:
  1.3 44.2 %shard_map.58 = (f32[86,768]{1,0:T(8,128)S(1)}, f32[86,768]{1,0:T(8,128)S(1)}, f32[1,3072]{1,0:T(1,128)S(1)}) custom-call(s32[1]{0:T(128)S(6)} %copy.6.rc_ref, s32[1,3072]{1,0:T(1,128)} %bitcast.2, bf16[3072,768]{1,0:T(8,128)(2,1)} %e_hbm.1), custom_call_target="tpu_custom_call" | custom-call | tf_op jit(solution)/shard_map/pallas_call | solution.py:407
  45.5 0.8 %shard_map.59 = (f32[86,768]{1,0:T(8,128)}, f32[86,768]{1,0:T(8,128)}, f32[1,3072]{1,0:T(1,128)}) custom-call(f32[86,768]{1,0:T(8,128)S(1)} %get-tuple-element.9.means_ref, f32[86,768]{1,0:T(8,128)S(1)} %get-tuple-element.10.proto_ref, f32[1,3072]{1,0:T(1,128)S(1)} %get-tuple-element.11.sim_ref), custom_call_target="tpu_custom_call" | custom-call | tf_op jit(solution)/shard_map/pallas_call | solution.py:446

commit v4 on v3

--- a/solution.py
+++ b/solution.py
@@ -23,8 +23,11 @@
 HALF = PEERS // 2
 GROUPS = ((7, 5, 6, 4, 3, 1, 2), (11, 15, 9, 13, 10, 14, 8, 12))
 ORDER = (7, 11, 15, 5, 6, 3, 9, 13, 10, 14, 4, 8, 12, 1, 2)
-CHUNK = 256
-SECOND_AT = ((), (0,), (1, 2), ())
+CUTS = (0, 256, 512, 768)
+CUTS3 = (0, 256, 768)
+SECOND_AT = ((), (0,), (1, 2))
+TAKE = ((0, 0), (0, 1), (1, 0), (0, 2))
+TAKE_LATE = ((1, 1), (1, 2))
 STEP = 512
 
 NN = ((1,), (0,))
@@ -89,7 +92,7 @@
     sim_rsem,
 ):
     rows, width = e_ref.shape
-    chunks = width // CHUNK
+    chunks, chunks3 = len(CUTS) - 1, len(CUTS3) - 1
     dp, cls = lax.axis_index("dp"), lax.axis_index("cls")
     x, z_lo = dp // 4, dp % 4
     y, z_hi, core = cls // 4, (cls // 2) % 2, cls % 2
@@ -109,11 +112,14 @@
 
     far = device(x, y, (z + 4) % Z, core)
 
+    def columns(f, cuts=CUTS):
+        return slice(cuts[f], cuts[f + 1])
+
     smalls = [pltpu.make_async_copy(lab_hbm, lab_ref, small_sem.at[0])]
     loads = [
         pltpu.make_async_copy(
-            e_hbm.at[:, pl.ds(f * CHUNK, CHUNK)],
-            e_ref.at[:, pl.ds(f * CHUNK, CHUNK)],
+            e_hbm.at[:, columns(f)],
+            e_ref.at[:, columns(f)],
             e_sem.at[f],
         )
         for f in range(chunks)
@@ -122,18 +128,11 @@
         load.start()
 
     barrier = pltpu.get_barrier_semaphore()
-    greeted = 0
-    for dx in range(X):
-        for dz in range(-2, 3):
-            if (dx, dz) != (0, 0):
-                pl.semaphore_signal(barrier, inc=1, device_id=at_offset(dx, dz), device_id_type=MESH)
-                greeted += 1
-    for dy, dc in fan:
-        pl.semaphore_signal(barrier, inc=1, device_id=fan_device(dy, dc), device_id_type=MESH)
-        greeted += 1
-    pl.semaphore_signal(barrier, inc=1, device_id=far, device_id_type=MESH)
-    greeted += 1
-
+    plane = [(dx, dz) for dx in range(X) for dz in range(-2, 3) if (dx, dz) != (0, 0)]
+    plane.sort(key=lambda at: -min(at[0], X - at[0]) - abs(at[1]))
+    greeted = [far] + [at_offset(*at) for at in plane] + [fan_device(*at) for at in fan]
+    for other in greeted:
+        pl.semaphore_signal(barrier, inc=1, device_id=other, device_id_type=MESH)
     for load in loads:
         load.start()
 
@@ -167,8 +166,8 @@
     slot = jnp.where(owned, peer * SLOTS + rank_row.astype(jnp.int32), -1)
 
     for k in range(PEERS):
-        meta_out[k] = jnp.broadcast_to(counts[k : k + 1], (8, LANES))
-    meta_in[0] = jnp.broadcast_to(counts[0:1], (8, LANES))
+        meta_out[k] = counts[k : k + 1]
+    meta_in[0] = counts[0:1]
 
     slot_iota = lax.broadcasted_iota(jnp.int32, (TABLE, STEP), 0)
     for n in range(rows // STEP):
@@ -181,8 +180,8 @@
         source, target = ((out1, in1), (out2, in2), (out3, in3))[phase]
         to = at_offset(-DX[k], -DZ[k]) if phase == 1 else at_offset(DX[k], DZ[k])
         move = pltpu.make_async_remote_copy(
-            src_ref=source.at[f, pl.ds(k * SLOTS, SLOTS)],
-            dst_ref=target.at[f, pl.ds(k * SLOTS, SLOTS)],
+            src_ref=source.at[pl.ds(k * SLOTS, SLOTS), columns(f, CUTS3 if phase == 2 else CUTS)],
+            dst_ref=target.at[pl.ds(k * SLOTS, SLOTS), columns(f, CUTS3 if phase == 2 else CUTS)],
             send_sem=ssem.at[phase, f, k],
             recv_sem=rsem.at[phase, f, k],
             device_id=to,
@@ -195,33 +194,31 @@
         for k in peers:
             moves[phase, f, k].wait_recv()
 
-    def columns(f):
-        return pl.ds(f * CHUNK, CHUNK)
-
-    def segment_sums(slots, f):
-        return dot(hot_ref[slots, :], e_ref[:, columns(f)], NN)
+    def segment_sums(slots, f, cuts=CUTS):
+        return dot(hot_ref[slots, :], e_ref[:, columns(f, cuts)], NN)
 
     loads[0].wait()
-    out1[0] = segment_sums(slice(0, TABLE), 0)
-    pl.semaphore_wait(barrier, greeted)
-    metas = {}
-    for k in ORDER:
-        metas[k] = pltpu.make_async_remote_copy(
-            src_ref=meta_out.at[k],
-            dst_ref=meta_in.at[k],
-            send_sem=meta_ssem.at[k],
-            recv_sem=meta_rsem.at[k],
-            device_id=at_offset(DX[k], DZ[k]),
-            device_id_type=MESH,
-        )
-        metas[k].start()
+    out1[:, columns(0)] = segment_sums(slice(0, TABLE), 0)
+    pl.semaphore_wait(barrier, len(greeted))
     for f in range(chunks):
         if f > 0:
             loads[f].wait()
-            out1[f] = segment_sums(slice(0, TABLE), f)
-        in1[f, 0:SLOTS] = out1[f, 0:SLOTS]
+            out1[:, columns(f)] = segment_sums(slice(0, TABLE), f)
+        in1[0:SLOTS, columns(f)] = out1[0:SLOTS, columns(f)]
         for k in ORDER:
             send(0, f, k)
+        if f == 0:
+            metas = {}
+            for k in ORDER:
+                metas[k] = pltpu.make_async_remote_copy(
+                    src_ref=meta_out.at[k],
+                    dst_ref=meta_in.at[k],
+                    send_sem=meta_ssem.at[k],
+                    recv_sem=meta_rsem.at[k],
+                    device_id=at_offset(DX[k], DZ[k]),
+                    device_id_type=MESH,
+                )
+                metas[k].start()
 
     ones = jnp.ones((8, LANES), BF16)
     for n in range(rows // STEP):
@@ -235,7 +232,7 @@
 
     for k in ORDER:
         metas[k].wait()
-    counts8 = meta_in[...].reshape(PEERS * 8, LANES)
+    counts8 = jnp.concatenate([jnp.broadcast_to(meta_in[k], (8, LANES)) for k in range(PEERS)], axis=0)
     present8 = counts8 > 0
     rank8 = jnp.where(present8, ranks(jnp.where(present8, 1.0, 0.0)), -1.0).reshape(PEERS, 8, LANES)
     at8 = lax.broadcasted_iota(jnp.int32, (PEERS, 8, LANES), 1).astype(F32)
@@ -250,13 +247,13 @@
 
     for f in range(chunks):
         receive(0, f, ORDER)
-        sums = sum(dot(turned_ref[...], piece, NN) for piece in split(in1[f], 3))
+        sums = sum(dot(turned_ref[...], piece, NN) for piece in split(in1[:, columns(f)], 3))
         means = jnp.concatenate(
-            [sums[:, j * LANES : (j + 1) * LANES] * inverse for j in range(CHUNK // LANES)], axis=1
+            [sums[:, j * LANES : (j + 1) * LANES] * inverse for j in range(sums.shape[1] // LANES)], axis=1
         )
         means_ref[:, columns(f)] = means[0:CLS_DEV]
-        out2[f] = sum(dot(map_ref[...], piece, NN) for piece in split(means, 2))
-        in2[f, 0:SLOTS] = out2[f, 0:SLOTS]
+        out2[:, columns(f)] = sum(dot(map_ref[...], piece, NN) for piece in split(means, 2))
+        in2[0:SLOTS, columns(f)] = out2[0:SLOTS, columns(f)]
         for k in GROUPS[0]:
             send(1, f, k)
         for late in SECOND_AT[f]:
@@ -264,16 +261,14 @@
                 send(1, late, k)
 
     def products(g, f, n):
-        high, low = split(in2[f, pl.ds(g * LANES, LANES)], 2)
+        high, low = split(in2[pl.ds(g * LANES, LANES), columns(f)], 2)
         both = jnp.concatenate([high, low], axis=0)
         found = dot(both, e_ref[pl.ds(n * STEP, STEP), columns(f)], NT)
         return found[0:LANES] + found[LANES:]
 
     def weigh(g):
-        square = sum(
-            jnp.sum(in2[f, pl.ds(g * LANES, LANES)] * in2[f, pl.ds(g * LANES, LANES)], axis=1, keepdims=True)
-            for f in range(chunks)
-        )
+        means = in2[pl.ds(g * LANES, LANES), :]
+        square = jnp.sum(means * means, axis=1, keepdims=True)
         scale = 1.0 / jnp.sqrt(square + EPSILON)
         iota = lax.broadcasted_iota(jnp.int32, (LANES, STEP), 0) + g * LANES
         for n in range(rows // STEP):
@@ -294,9 +289,9 @@
 
     def weighted_sums(g, f):
         own = slice(g * LANES, (g + 1) * LANES)
-        out3[f, own] = segment_sums(own, f)
+        out3[own, columns(f, CUTS3)] = segment_sums(own, f, CUTS3)
         if g == 0:
-            in3[f, 0:SLOTS] = out3[f, 0:SLOTS]
+            in3[0:SLOTS, columns(f, CUTS3)] = out3[0:SLOTS, columns(f, CUTS3)]
         for k in GROUPS[g]:
             send(2, f, k)
 
@@ -310,17 +305,12 @@
                 found = products(g, f, n)
                 score_ref[g, :, at] = found if f == 0 else score_ref[g, :, at] + found
 
-    gather(0, 0)
-    gather(0, 1)
-    for late in SECOND_AT[chunks]:
-        for k in GROUPS[1]:
-            send(1, late, k)
-    gather(1, 0)
-    gather(0, 2)
-    for f in range(chunks):
+    for g, f in TAKE:
+        gather(g, f)
+    for f in range(chunks3):
         weighted_sums(0, f)
-    gather(1, 1)
-    gather(1, 2)
+    for g, f in TAKE_LATE:
+        gather(g, f)
 
     cut = rows // 8
     for j in range(8):
@@ -337,9 +327,8 @@
         )
         copy.start()
         spread.append(copy)
-    weighted_sums(1, 0)
-    weighted_sums(1, 1)
-    weighted_sums(1, 2)
+    for f in range(chunks3):
+        weighted_sums(1, f)
     for copy in spread:
         copy.wait()
     half = sim_own[...]
@@ -356,27 +345,32 @@
     )
     across.start()
 
+    for (phase, f, k), move in moves.items():
+        if phase < 2:
+            move.wait_send()
+
     def merged(g, f):
         receive(2, f, GROUPS[g])
         own = pl.ds(g * LANES, LANES)
-        return sum(dot(turned_ref[:, own], piece, NN) for piece in split(in3[f, own], 3))
-
-    for f in range(chunks):
-        score_ref[0, :, columns(f)] = merged(0, f)
+        return sum(dot(turned_ref[:, own], piece, NN) for piece in split(in3[own, columns(f, CUTS3)], 3))
+
+    for f in range(chunks3):
+        score_ref[0, :, columns(f, CUTS3)] = merged(0, f)
     weighted = []
-    for f in range(chunks):
-        weighted.append(score_ref[0, :, columns(f)] + merged(1, f))
+    for f in range(chunks3):
+        weighted.append(score_ref[0, :, columns(f, CUTS3)] + merged(1, f))
     square = sum(jnp.sum(piece * piece, axis=1, keepdims=True) for piece in weighted)
     norm = 1.0 / jnp.sqrt(square + EPSILON)
-    for f in range(chunks):
-        proto_ref[:, columns(f)] = (weighted[f] * norm)[0:CLS_DEV]
+    for f in range(chunks3):
+        proto_ref[:, columns(f, CUTS3)] = (weighted[f] * norm)[0:CLS_DEV]
 
     across.wait()
     both = sim_half[...] + sim_far[...]
     for j in range(8):
         sim_ref[:, pl.ds(j * cut, cut)] = both[j : j + 1, :]
-    for move in moves.values():
-        move.wait_send()
+    for (phase, f, k), move in moves.items():
+        if phase == 2:
+            move.wait_send()
 
 
 def writer(means_ref, proto_ref, sim_ref, means_hbm, proto_hbm, sim_hbm, sem):
@@ -393,11 +387,11 @@
 
 def shards(embeddings, labels, row_count):
     rows, width = embeddings.shape
-    chunks = width // CHUNK
+    chunks = max(len(CUTS), len(CUTS3)) - 1
     vmem = pl.BlockSpec(memory_space=pltpu.VMEM)
     anywhere = pl.BlockSpec(memory_space=pl.ANY)
     hbm = pl.BlockSpec(memory_space=pltpu.MemorySpace.HBM)
-    table = pltpu.VMEM((chunks, TABLE, CHUNK), F32)
+    table = pltpu.VMEM((TABLE, width), F32)
     line = (8, rows // 8)
     shapes = ((CLS_DEV, width), (CLS_DEV, width), (1, rows))
     inputs = [row_count] + [
@@ -413,8 +407,8 @@
             pltpu.VMEM((1, rows), jnp.int32),
             pltpu.VMEM((rows, width), BF16),
             pltpu.VMEM((TABLE, rows), BF16),
-            pltpu.VMEM((PEERS, 8, LANES), F32),
-            pltpu.VMEM((PEERS, 8, LANES), F32),
+            pltpu.VMEM((PEERS, 1, LANES), F32),
+            pltpu.VMEM((PEERS, 1, LANES), F32),
             table,
             table,
             table,

time: 46.5 us -> 45.7 us (0.983)
  Pallas kernels: 45 us -> 44.2 us
    pallas_call x1, Pallas kernels: 44.2 us -> 43.4 us  [shards(): pl.pallas_call(kernel, out_shape=tuple((pltpu.VMEM(shape, F32) for shape...]
where the time goes in v4:
time: 45.7 us; the launch traced here: 45.5 us
  Pallas kernels  44.2 us (97%)
  between operations  1.28 us (3%)
    pallas_call x1, Pallas kernels, shards(): pl.pallas_call(kernel, out_shape=tuple((pltpu.VMEM(shape, F32) for shape...  43.4 us

profile of v4, /device:TPU:1, one launch (start us, length us, event | category | flops | bytes accessed | tf_op | source)
XLA Modules:
  0.0 45.5 jit_solution(12258232281280021182)
XLA Ops:
  1.3 43.4 %shard_map.58 = (f32[86,768]{1,0:T(8,128)S(1)}, f32[86,768]{1,0:T(8,128)S(1)}, f32[1,3072]{1,0:T(1,128)S(1)}) custom-call(s32[1]{0:T(128)S(6)} %copy.6.rc_ref, s32[1,3072]{1,0:T(1,128)} %bitcast.2, bf16[3072,768]{1,0:T(8,128)(2,1)} %e_hbm.1), custom_call_target="tpu_custom_call" | custom-call | tf_op jit(solution)/shard_map/pallas_call | solution.py:401
  44.7 0.8 %shard_map.59 = (f32[86,768]{1,0:T(8,128)}, f32[86,768]{1,0:T(8,128)}, f32[1,3072]{1,0:T(1,128)}) custom-call(f32[86,768]{1,0:T(8,128)S(1)} %get-tuple-element.9.means_ref, f32[86,768]{1,0:T(8,128)S(1)} %get-tuple-element.10.proto_ref, f32[1,3072]{1,0:T(1,128)S(1)} %get-tuple-element.11.sim_ref), custom_call_target="tpu_custom_call" | custom-call | tf_op jit(solution)/shard_map/pallas_call | solution.py:440

commit v5 on v4

--- a/solution.py
+++ b/solution.py
@@ -174,25 +174,32 @@
         hit = slot[:, n * STEP : (n + 1) * STEP] == slot_iota
         hot_ref[:, pl.ds(n * STEP, STEP)] = jnp.where(hit, 1.0, 0.0).astype(BF16)
 
-    moves = {}
-
     def send(phase, f, k):
         source, target = ((out1, in1), (out2, in2), (out3, in3))[phase]
         to = at_offset(-DX[k], -DZ[k]) if phase == 1 else at_offset(DX[k], DZ[k])
         move = pltpu.make_async_remote_copy(
             src_ref=source.at[pl.ds(k * SLOTS, SLOTS), columns(f, CUTS3 if phase == 2 else CUTS)],
             dst_ref=target.at[pl.ds(k * SLOTS, SLOTS), columns(f, CUTS3 if phase == 2 else CUTS)],
-            send_sem=ssem.at[phase, f, k],
-            recv_sem=rsem.at[phase, f, k],
+            send_sem=ssem.at[phase, f, k // HALF],
+            recv_sem=rsem.at[phase, f, k // HALF],
             device_id=to,
             device_id_type=MESH,
         )
         move.start()
-        moves[phase, f, k] = move
-
-    def receive(phase, f, peers):
-        for k in peers:
-            moves[phase, f, k].wait_recv()
+
+    def all_of(sem, array, phase, f, g):
+        first = max(g * HALF, 1) * SLOTS
+        span = array.at[first : (g + 1) * HALF * SLOTS, columns(f, CUTS3 if phase == 2 else CUTS)]
+        pltpu.make_async_copy(span, span, sem.at[phase, f, g]).wait()
+
+    def receive(phase, f, g):
+        all_of(rsem, (in1, in2, in3)[phase], phase, f, g)
+
+    def sent(phases):
+        for phase in phases:
+            for f in range(chunks3 if phase == 2 else chunks):
+                for g in range(2):
+                    all_of(ssem, (out1, out2, out3)[phase], phase, f, g)
 
     def segment_sums(slots, f, cuts=CUTS):
         return dot(hot_ref[slots, :], e_ref[:, columns(f, cuts)], NN)
@@ -213,8 +220,8 @@
                 metas[k] = pltpu.make_async_remote_copy(
                     src_ref=meta_out.at[k],
                     dst_ref=meta_in.at[k],
-                    send_sem=meta_ssem.at[k],
-                    recv_sem=meta_rsem.at[k],
+                    send_sem=meta_ssem.at[0],
+                    recv_sem=meta_rsem.at[0],
                     device_id=at_offset(DX[k], DZ[k]),
                     device_id_type=MESH,
                 )
@@ -230,8 +237,9 @@
         total = sum(dot(ones, piece, NT) for piece in split(lanes, 3))
         part_ref[0:1, pl.ds(n * STEP, STEP)] = 1.0 / jnp.sqrt(total[0:1] + EPSILON)
 
-    for k in ORDER:
-        metas[k].wait()
+    for sem, array in ((meta_ssem, meta_out), (meta_rsem, meta_in)):
+        span = array.at[1:PEERS]
+        pltpu.make_async_copy(span, span, sem.at[0]).wait()
     counts8 = jnp.concatenate([jnp.broadcast_to(meta_in[k], (8, LANES)) for k in range(PEERS)], axis=0)
     present8 = counts8 > 0
     rank8 = jnp.where(present8, ranks(jnp.where(present8, 1.0, 0.0)), -1.0).reshape(PEERS, 8, LANES)
@@ -246,7 +254,8 @@
     inverse = 1.0 / jnp.maximum(counted, 1.0)
 
     for f in range(chunks):
-        receive(0, f, ORDER)
+        receive(0, f, 0)
+        receive(0, f, 1)
         sums = sum(dot(turned_ref[...], piece, NN) for piece in split(in1[:, columns(f)], 3))
         means = jnp.concatenate(
             [sums[:, j * LANES : (j + 1) * LANES] * inverse for j in range(sums.shape[1] // LANES)], axis=1
@@ -296,7 +305,7 @@
             send(2, f, k)
 
     def gather(g, f):
-        receive(1, f, GROUPS[g])
+        receive(1, f, g)
         if f == chunks - 1:
             weigh(g)
         else:
@@ -345,12 +354,10 @@
     )
     across.start()
 
-    for (phase, f, k), move in moves.items():
-        if phase < 2:
-            move.wait_send()
+    sent((0, 1))
 
     def merged(g, f):
-        receive(2, f, GROUPS[g])
+        receive(2, f, g)
         own = pl.ds(g * LANES, LANES)
         return sum(dot(turned_ref[:, own], piece, NN) for piece in split(in3[own, columns(f, CUTS3)], 3))
 
@@ -368,9 +375,7 @@
     both = sim_half[...] + sim_far[...]
     for j in range(8):
         sim_ref[:, pl.ds(j * cut, cut)] = both[j : j + 1, :]
-    for (phase, f, k), move in moves.items():
-        if phase == 2:
-            move.wait_send()
+    sent((2,))
 
 
 def writer(means_ref, proto_ref, sim_ref, means_hbm, proto_hbm, sim_hbm, sem):
@@ -425,10 +430,10 @@
             pltpu.VMEM(line, F32),
             pltpu.SemaphoreType.DMA((2,)),
             pltpu.SemaphoreType.DMA((chunks,)),
-            pltpu.SemaphoreType.DMA((PEERS,)),
-            pltpu.SemaphoreType.DMA((PEERS,)),
-            pltpu.SemaphoreType.DMA((3, chunks, PEERS)),
-            pltpu.SemaphoreType.DMA((3, chunks, PEERS)),
+            pltpu.SemaphoreType.DMA((1,)),
+            pltpu.SemaphoreType.DMA((1,)),
+            pltpu.SemaphoreType.DMA((3, chunks, 2)),
+            pltpu.SemaphoreType.DMA((3, chunks, 2)),
             pltpu.SemaphoreType.DMA((8,)),
             pltpu.SemaphoreType.DMA((8,)),
         ],

time: 45.7 us -> 43 us (0.941)
  Pallas kernels: 44.2 us -> 41.5 us
    pallas_call x1, Pallas kernels: 43.4 us -> 40.7 us  [shards(): pl.pallas_call(kernel, out_shape=tuple((pltpu.VMEM(shape, F32) for shape...]
where the time goes in v5:
time: 43 us; the launch traced here: 42.8 us
  Pallas kernels  41.5 us (97%)
  between operations  1.28 us (3%)
    pallas_call x1, Pallas kernels, shards(): pl.pallas_call(kernel, out_shape=tuple((pltpu.VMEM(shape, F32) for shape...  40.7 us

profile of v5, /device:TPU:1, one launch (start us, length us, event | category | flops | bytes accessed | tf_op | source)
XLA Modules:
  0.0 42.8 jit_solution(800543637028050201)
XLA Ops:
  1.3 40.7 %shard_map.58 = (f32[86,768]{1,0:T(8,128)S(1)}, f32[86,768]{1,0:T(8,128)S(1)}, f32[1,3072]{1,0:T(1,128)S(1)}) custom-call(s32[1]{0:T(128)S(6)} %copy.6.rc_ref, s32[1,3072]{1,0:T(1,128)} %bitcast.2, bf16[3072,768]{1,0:T(8,128)(2,1)} %e_hbm.1), custom_call_target="tpu_custom_call" | custom-call | tf_op jit(solution)/shard_map/pallas_call | solution.py:406
  42.0 0.8 %shard_map.59 = (f32[86,768]{1,0:T(8,128)}, f32[86,768]{1,0:T(8,128)}, f32[1,3072]{1,0:T(1,128)}) custom-call(f32[86,768]{1,0:T(8,128)S(1)} %get-tuple-element.9.means_ref, f32[86,768]{1,0:T(8,128)S(1)} %get-tuple-element.10.proto_ref, f32[1,3072]{1,0:T(1,128)S(1)} %get-tuple-element.11.sim_ref), custom_call_target="tpu_custom_call" | custom-call | tf_op jit(solution)/shard_map/pallas_call | solution.py:445

commit v6 on v5

--- a/solution.py
+++ b/solution.py
@@ -324,22 +324,20 @@
     cut = rows // 8
     for j in range(8):
         sim_own[j : j + 1, :] = part_ref[1:2, pl.ds(j * cut, cut)]
-    spread = []
     for n, (dy, dc) in enumerate(fan):
         copy = pltpu.make_async_remote_copy(
             src_ref=sim_own,
             dst_ref=sim_in.at[n],
-            send_sem=sim_ssem.at[n],
-            recv_sem=sim_rsem.at[n],
+            send_sem=sim_ssem.at[0],
+            recv_sem=sim_rsem.at[0],
             device_id=fan_device(dy, dc),
             device_id_type=MESH,
         )
         copy.start()
-        spread.append(copy)
     for f in range(chunks3):
         weighted_sums(1, f)
-    for copy in spread:
-        copy.wait()
+    for sem in (sim_ssem, sim_rsem):
+        pltpu.make_async_copy(sim_in, sim_in, sem.at[0]).wait()
     half = sim_own[...]
     for n in range(len(fan)):
         half = half + sim_in[n]
@@ -347,8 +345,8 @@
     across = pltpu.make_async_remote_copy(
         src_ref=sim_half,
         dst_ref=sim_far,
-        send_sem=sim_ssem.at[7],
-        recv_sem=sim_rsem.at[7],
+        send_sem=sim_ssem.at[1],
+        recv_sem=sim_rsem.at[1],
         device_id=far,
         device_id_type=MESH,
     )
@@ -434,8 +432,8 @@
             pltpu.SemaphoreType.DMA((1,)),
             pltpu.SemaphoreType.DMA((3, chunks, 2)),
             pltpu.SemaphoreType.DMA((3, chunks, 2)),
-            pltpu.SemaphoreType.DMA((8,)),
-            pltpu.SemaphoreType.DMA((8,)),
+            pltpu.SemaphoreType.DMA((2,)),
+            pltpu.SemaphoreType.DMA((2,)),
         ],
         compiler_params=pltpu.CompilerParams(
             collective_id=0, has_side_effects=True, vmem_limit_bytes=48 * 1024 * 1024

time: 43 us -> 42.9 us (level)
  no operation moved by 1% of the time
where the time goes in v6:
time: 42.9 us; the launch traced here: 42.7 us
  Pallas kernels  41.4 us (97%)
  between operations  1.28 us (3%)
    pallas_call x1, Pallas kernels, shards(): pl.pallas_call(kernel, out_shape=tuple((pltpu.VMEM(shape, F32) for shape...  40.6 us

profile of v6, /device:TPU:1, one launch (start us, length us, event | category | flops | bytes accessed | tf_op | source)
XLA Modules:
  0.0 42.7 jit_solution(4102659969648745312)
XLA Ops:
  1.3 40.6 %shard_map.58 = (f32[86,768]{1,0:T(8,128)S(1)}, f32[86,768]{1,0:T(8,128)S(1)}, f32[1,3072]{1,0:T(1,128)S(1)}) custom-call(s32[1]{0:T(128)S(6)} %copy.6.rc_ref, s32[1,3072]{1,0:T(1,128)} %bitcast.2, bf16[3072,768]{1,0:T(8,128)(2,1)} %e_hbm.1), custom_call_target="tpu_custom_call" | custom-call | tf_op jit(solution)/shard_map/pallas_call | solution.py:404
  41.9 0.8 %shard_map.59 = (f32[86,768]{1,0:T(8,128)}, f32[86,768]{1,0:T(8,128)}, f32[1,3072]{1,0:T(1,128)}) custom-call(f32[86,768]{1,0:T(8,128)S(1)} %get-tuple-element.9.means_ref, f32[86,768]{1,0:T(8,128)S(1)} %get-tuple-element.10.proto_ref, f32[1,3072]{1,0:T(1,128)S(1)} %get-tuple-element.11.sim_ref), custom_call_target="tpu_custom_call" | custom-call | tf_op jit(solution)/shard_map/pallas_call | solution.py:443
